TPU v7x, 32 devices: a whole 2x2x4 slice. The times are simulated.
32 devices in a mesh: dp: 8 (over z, y), fsdp: 4 (over x, core).
Axes of the slice: x: 2, y: 2, z: 4, core: 2. Of those that a mesh axis runs over, the one named last changes fastest.
Arguments:
- tokens: bfloat16 [65536, 384], P(('dp', 'fsdp')), may hold values from -6 to 6
- cotangent: bfloat16 [65536, 384], P(('dp', 'fsdp')), may hold values from -6 to 6
- image_lengths: int32 [32, 112], P(('dp', 'fsdp')), may hold values from 0 to 66, as said below
- segment_ids: int32 [65536], P(('dp', 'fsdp')), may hold values from 0 to 112, as said below
- w_qkv: bfloat16 [442368], P(('dp', 'fsdp')), may hold values from -0.3125 to 0.3125
- w_out: bfloat16 [147456], P(('dp', 'fsdp')), may hold values from -1.75 to 1.75
- w_up: bfloat16 [589824], P(('dp', 'fsdp')), may hold values from -0.3125 to 0.3125
- w_down: bfloat16 [589824], P(('dp', 'fsdp')), may hold values from -0.15625 to 0.15625
- small_params: bfloat16 [4608], P(('dp', 'fsdp'))
Outputs:
- output: bfloat16 [65536, 384], P(('dp', 'fsdp'))
- input_grad: bfloat16 [65536, 384], P(('dp', 'fsdp'))
- grad_qkv: float32 [442368], P(('dp', 'fsdp'))
- grad_out: float32 [147456], P(('dp', 'fsdp'))
- grad_up: float32 [589824], P(('dp', 'fsdp'))
- grad_down: float32 [589824], P(('dp', 'fsdp'))
- grad_small: float32 [4608], P(('dp', 'fsdp'))
Inputs may be any that keep to these rules, and one draw needn't show every extreme that they name: `image_lengths`: row p lists pack p's images in order, then zeros. The first image of every pack has 66 tokens, and every other image but a pack's last has 18 tokens or more. A pack's lengths sum to at least 1843 and below 2048, except in one pack, which holds 112 images and sums to 2048. `segment_ids`: token t of pack p carries the number of pack p's images that end at or before t; padding after the last image carries 112.
All inputs are finite; a program needn't handle non-finite values.
Results may differ from a plain program's by a relative error of at most 0.011.
Values may be sent and summed in bfloat16 or wider, within the bound.
A program may use at most 128 MiB of HBM per device.

v0:
```python
import jax
import jax.numpy as jnp
from jax import lax
from jax.sharding import PartitionSpec as P

HEADS = 6
HEAD_DIM = 64
FF = 1536
MAX_IMG = 66


norm_eps = 1e-06
masked_score = -1e30


def layer_norm(inputs, gain, shift):
    center = jnp.mean(inputs, axis=-1, keepdims=True)
    offset = inputs - center
    spread = jnp.mean(offset * offset, axis=-1, keepdims=True)
    return offset * lax.rsqrt(spread + norm_eps) * gain + shift


def exact_gelu(upward):
    return jax.nn.gelu(upward, approximate=False)


def split_small(small_all):
    model_width = HEADS * HEAD_DIM
    pieces = tuple(
        (small_all[member * model_width : (member + 1) * model_width] for member in range(8))
    )
    return pieces + (small_all[8 * model_width :],)


def unpack_matrices(flat_qkv, flat_out, flat_up, flat_down):
    model_width = HEADS * HEAD_DIM
    return (
        flat_qkv.reshape(model_width, 3 * model_width),
        flat_out.reshape(model_width, model_width),
        flat_up.reshape(model_width, FF),
        flat_down.reshape(FF, model_width),
    )


def matmul_low(left_side, right_side):
    return jnp.dot(left_side, right_side, preferred_element_type=jnp.float32)


def contract_rows(left_side, right_side):
    return lax.dot_general(
        left_side, right_side, (((0,), (0,)), ((), ())), preferred_element_type=jnp.float32
    )


def contract_cols(left_side, right_side):
    return lax.dot_general(
        left_side, right_side, (((1,), (1,)), ((), ())), preferred_element_type=jnp.float32
    )


def add_window(total, part_sum, window_start):
    window_rows = part_sum.shape[0]
    current = lax.dynamic_slice_in_dim(total, window_start, window_rows, 0)
    return lax.dynamic_update_slice_in_dim(total, current + part_sum, window_start, 0)


def local(tokens, cotangent, image_lengths, segment_ids, w_qkv, w_out, w_up, w_down, small_params):
    model_width = HEADS * HEAD_DIM
    score_scale = HEAD_DIM ** (-0.5)
    rows_count = tokens.shape[0]
    block_rows = min(512, rows_count)
    blocks_count = rows_count // block_rows
    margin = 128 * ((MAX_IMG + 127) // 128)
    window_rows = min(rows_count, block_rows + 2 * margin)
    window_starts = jnp.clip(
        jnp.arange(blocks_count, dtype=jnp.int32) * block_rows - margin, 0, rows_count - window_rows
    )
    fetched = (
        lax.all_gather(w_qkv, ("dp", "fsdp"), axis=0, tiled=True),
        lax.all_gather(w_out, ("dp", "fsdp"), axis=0, tiled=True),
        lax.all_gather(w_up, ("dp", "fsdp"), axis=0, tiled=True),
        lax.all_gather(w_down, ("dp", "fsdp"), axis=0, tiled=True),
        lax.all_gather(small_params, ("dp", "fsdp"), axis=0, tiled=True),
    )
    qkv_mat, out_mat, up_mat, down_mat = unpack_matrices(
        fetched[0], fetched[1], fetched[2], fetched[3]
    )
    small_all = fetched[4].astype(jnp.float32)
    gain_one, gain_two, bias_one, bias_two, bias_query, bias_value, bias_out, bias_down, bias_up = (
        split_small(small_all)
    )
    filled = (jnp.arange(rows_count, dtype=jnp.int32) < jnp.sum(image_lengths)).astype(jnp.float32)[
        :, None
    ]
    hidden_in = tokens.astype(jnp.float32)
    normed, norm_back_one = jax.vjp(layer_norm, hidden_in, gain_one, bias_one)
    normed_low = normed.astype(jnp.bfloat16)
    projected = matmul_low(normed_low, qkv_mat)
    queries = (
        (projected[:, :model_width] + bias_query)
        .astype(jnp.bfloat16)
        .reshape(rows_count, HEADS, HEAD_DIM)
    )
    keys_low = (
        projected[:, model_width : 2 * model_width]
        .astype(jnp.bfloat16)
        .reshape(rows_count, HEADS, HEAD_DIM)
    )
    values_low = (
        (projected[:, 2 * model_width :] + bias_value)
        .astype(jnp.bfloat16)
        .reshape(rows_count, HEADS, HEAD_DIM)
    )
    query_blocks = queries.reshape(blocks_count, block_rows, HEADS, HEAD_DIM)
    segment_blocks = segment_ids.reshape(blocks_count, block_rows)

    def scores_of(query_block, segment_block, window_start):
        key_window = lax.dynamic_slice_in_dim(keys_low, window_start, window_rows, 0)
        value_window = lax.dynamic_slice_in_dim(values_low, window_start, window_rows, 0)
        segment_window = lax.dynamic_slice_in_dim(segment_ids, window_start, window_rows, 0)
        scores_raw = (
            jnp.einsum("qhd,khd->hqk", query_block, key_window, preferred_element_type=jnp.float32)
            * score_scale
        )
        allowed = segment_block[:, None] == segment_window[None, :]
        return (jnp.where(allowed[None], scores_raw, masked_score), key_window, value_window)

    def attend(block_args):
        query_block, segment_block, window_start = block_args
        scores, key_window, value_window = scores_of(query_block, segment_block, window_start)
        peak = jnp.max(scores, axis=-1, keepdims=True)
        exponent = jnp.exp(scores - peak)
        denominator = jnp.sum(exponent, axis=-1, keepdims=True)
        probs_low = (exponent / denominator).astype(jnp.bfloat16)
        attended_block = jnp.einsum(
            "hqk,khd->qhd", probs_low, value_window, preferred_element_type=jnp.float32
        )
        return (attended_block.astype(jnp.bfloat16), peak[..., 0] + jnp.log(denominator[..., 0]))

    attended, log_totals = lax.map(attend, (query_blocks, segment_blocks, window_starts))
    attended = attended.reshape(rows_count, model_width)
    mixed = hidden_in + matmul_low(attended, out_mat) + bias_out
    normed_two, norm_back_two = jax.vjp(layer_norm, mixed, gain_two, bias_two)
    normed_two_low = normed_two.astype(jnp.bfloat16)
    upward = matmul_low(normed_two_low, up_mat) + bias_up
    activated, gelu_back = jax.vjp(exact_gelu, upward)
    activated_low = activated.astype(jnp.bfloat16)
    result = mixed + matmul_low(activated_low, down_mat) + bias_down
    output = (result * filled).astype(jnp.bfloat16)
    refetched = (
        lax.all_gather(w_qkv, ("dp", "fsdp"), axis=0, tiled=True),
        lax.all_gather(w_out, ("dp", "fsdp"), axis=0, tiled=True),
        lax.all_gather(w_up, ("dp", "fsdp"), axis=0, tiled=True),
        lax.all_gather(w_down, ("dp", "fsdp"), axis=0, tiled=True),
    )
    qkv_mat, out_mat, up_mat, down_mat = unpack_matrices(
        refetched[0], refetched[1], refetched[2], refetched[3]
    )
    upstream = cotangent.astype(jnp.float32) * filled
    bias_down_grad = jnp.sum(upstream, axis=0)
    upstream_low = upstream.astype(jnp.bfloat16)
    down_grad = contract_rows(activated_low, upstream_low)
    activated_grad = contract_cols(upstream_low, down_mat)
    (upward_grad,) = gelu_back(activated_grad)
    bias_up_grad = jnp.sum(upward_grad, axis=0)
    upward_low = upward_grad.astype(jnp.bfloat16)
    up_grad = contract_rows(normed_two_low, upward_low)
    normed_two_grad = contract_cols(upward_low, up_mat)
    mixed_from_norm, gain_two_grad, bias_two_grad = norm_back_two(normed_two_grad)
    mixed_grad = upstream + mixed_from_norm
    bias_out_grad = jnp.sum(mixed_grad, axis=0)
    mixed_low = mixed_grad.astype(jnp.bfloat16)
    out_grad = contract_rows(attended, mixed_low)
    attended_grad = contract_cols(mixed_low, out_mat).astype(jnp.bfloat16)
    attended_grad = attended_grad.reshape(blocks_count, block_rows, HEADS, HEAD_DIM)

    def attend_back(carry, block_args):
        key_sum, value_sum = carry
        query_block, segment_block, upstream_block, log_block, window_start = block_args
        scores, key_window, value_window = scores_of(query_block, segment_block, window_start)
        probs = jnp.exp(scores - log_block[..., None])
        probs_low = probs.astype(jnp.bfloat16)
        probs_grad = jnp.einsum(
            "qhd,khd->hqk", upstream_block, value_window, preferred_element_type=jnp.float32
        )
        scores_grad = probs * (probs_grad - jnp.sum(probs * probs_grad, axis=-1, keepdims=True))
        scores_low = scores_grad.astype(jnp.bfloat16)
        query_grad_block = (
            jnp.einsum("hqk,khd->qhd", scores_low, key_window, preferred_element_type=jnp.float32)
            * score_scale
        )
        key_part = (
            jnp.einsum("hqk,qhd->khd", scores_low, query_block, preferred_element_type=jnp.float32)
            * score_scale
        )
        value_part = jnp.einsum(
            "hqk,qhd->khd", probs_low, upstream_block, preferred_element_type=jnp.float32
        )
        key_sum = add_window(key_sum, key_part, window_start)
        value_sum = add_window(value_sum, value_part, window_start)
        return ((key_sum, value_sum), query_grad_block)

    empty_grad = jnp.zeros((rows_count, HEADS, HEAD_DIM), jnp.float32)
    (key_grad, value_grad), query_grad = lax.scan(
        attend_back,
        (empty_grad, empty_grad),
        (query_blocks, segment_blocks, attended_grad, log_totals, window_starts),
    )
    query_grad = query_grad.reshape(rows_count, model_width)
    key_grad = key_grad.reshape(rows_count, model_width)
    value_grad = value_grad.reshape(rows_count, model_width)
    bias_query_grad = jnp.sum(query_grad, axis=0)
    bias_value_grad = jnp.sum(value_grad, axis=0)
    projected_low = jnp.concatenate([query_grad, key_grad, value_grad], axis=1).astype(jnp.bfloat16)
    qkv_grad = contract_rows(normed_low, projected_low)
    normed_grad = contract_cols(projected_low, qkv_mat)
    hidden_from_norm, gain_one_grad, bias_one_grad = norm_back_one(normed_grad)
    input_grad = (mixed_grad + hidden_from_norm).astype(jnp.bfloat16)
    small_grad = jnp.concatenate(
        [
            gain_one_grad,
            gain_two_grad,
            bias_one_grad,
            bias_two_grad,
            bias_query_grad,
            bias_value_grad,
            bias_out_grad,
            bias_down_grad,
            bias_up_grad,
        ]
    )
    qkv_share, out_share, up_share, down_share, small_share = (
        lax.psum_scatter(qkv_grad.reshape(-1), ("dp", "fsdp"), scatter_dimension=0, tiled=True),
        lax.psum_scatter(out_grad.reshape(-1), ("dp", "fsdp"), scatter_dimension=0, tiled=True),
        lax.psum_scatter(up_grad.reshape(-1), ("dp", "fsdp"), scatter_dimension=0, tiled=True),
        lax.psum_scatter(down_grad.reshape(-1), ("dp", "fsdp"), scatter_dimension=0, tiled=True),
        lax.psum_scatter(small_grad, ("dp", "fsdp"), scatter_dimension=0, tiled=True),
    )
    return (output, input_grad, qkv_share, out_share, up_share, down_share, small_share)


def solution(mesh):
    in_specs = (
        P(("dp", "fsdp"), None),
        P(("dp", "fsdp"), None),
        P(("dp", "fsdp"), None),
        P(("dp", "fsdp")),
        P(("dp", "fsdp")),
        P(("dp", "fsdp")),
        P(("dp", "fsdp")),
        P(("dp", "fsdp")),
        P(("dp", "fsdp")),
    )
    out_specs = (
        P(("dp", "fsdp"), None),
        P(("dp", "fsdp"), None),
        P(("dp", "fsdp")),
        P(("dp", "fsdp")),
        P(("dp", "fsdp")),
        P(("dp", "fsdp")),
        P(("dp", "fsdp")),
    )
    return jax.shard_map(local, mesh=mesh, in_specs=in_specs, out_specs=out_specs, check_vma=False)
```

profile of v0, /device:TPU:0, one launch (start us, length us, event | category | flops | bytes accessed | tf_op | source)
XLA Modules:
  0.0 688.7 jit_solution(11429810242576858687)
XLA Ops:
  9.6 42.3 %all-reduce = bf16[4608]{0:T(1024)(128)(2,1)S(1)} all-reduce(bf16[4608]{0:T(1024)(128)(2,1)S(1)} %dynamic-update-slice), channel_id=1, replica_groups=mesh['dp'=8,'fsdp'=4] {'dp','fsdp'}, use_global_device_ids=true, to_apply=%add | all-reduce | flops 4608 | bytes 18432
  57.2 42.1 %all-gather.1 = bf16[32,1,4608]{2,1,0:T(2,128)(2,1)S(1)} all-gather(bf16[1,1,4608]{2,1,0:T(2,128)(2,1)S(1)} %reshape.246), channel_id=1, replica_groups=mesh['dp'=8,'fsdp'=4] {'dp','fsdp'}, dimensions={0}, use_global_device_ids=true | all-gather | bytes 304128 | tf_op jit(solution)/shard_map/all_gather | solution.py:80
  106.6 42.1 %all-gather = bf16[32,1,13824]{2,1,0:T(2,128)(2,1)S(1)} all-gather(bf16[1,1,13824]{2,1,0:T(2,128)(2,1)S(1)} %reshape.244), channel_id=1, replica_groups=mesh['dp'=8,'fsdp'=4] {'dp','fsdp'}, dimensions={0}, use_global_device_ids=true | all-gather | bytes 912384 | tf_op jit(solution)/shard_map/all_gather | solution.py:79
  148.7 6.2 reduce.2
  166.4 54.2 %while.26 = (s32[]{:T(128)}, bf16[4,512,6,64]{1,3,2,0:T(8,128)(2,1)}, f32[4,6,512]{2,1,0:T(8,128)}, s32[4]{0:T(128)S(1)}, bf16[2048,6,64]{0,2,1:T(8,128)(2,1)}, ...) while((s32[]{:T(128)}, ...), condition=%wide.region_5.6_spmd, body=%wide.region_2.5_spmd.sunk | while | flops 632878080 | bytes 31968456 | solution.py:140
  174.2 5.1 fusion.138
  187.7 5.1 fusion.138
  201.2 5.1 fusion.138
  214.7 5.1 fusion.138
  231.1 34.7 %multiply_convert_fusion.1 = (bf16[2048,1536]{1,0:T(8,128)(2,1)}, f32[2048,1536]{1,0:T(8,128)}, f32[2048,1536]{1,0:T(8,128)}) fusion(f32[1536]{0:T(1024)S(1)} %slice.59, bf16[384,1536]{1,0:T(8,128)(2,1)} %reshape.232, f32[2048,384]{0,1:T(8,128)S(1)} %get-tuple-element.282, f32[384]{0:T(512)S(1)} %get-tuple-element.275, f32[384]{0:T(512)S(1)} %get-tuple-element.274, ...), kind=kOutput, calls=%fused_computation.61 | convolution fusion | flops 2627469312 | bytes 35808256 | tf_op jit(solution)/shard_map/dot_general | solution.py:46
  269.3 15.5 %fusion.102 = (f32[1536]{0:T(1024)}, bf16[2048,1536]{1,0:T(8,128)(2,1)S(1)}) fusion(f32[2048,1536]{1,0:T(8,128)} %get-tuple-element.261, bf16[1536,384]{1,0:T(8,128)(2,1)} %reshape.233, bf16[2048,384]{0,1:T(8,128)(2,1)} %copy.47, f32[2048]{0:T(1024)S(1)} %copy-done.35, f32[2048,1536]{1,0:T(8,128)} %get-tuple-element.283, f32[1536]{0:T(1024)S(1)} %slice.59), kind=kOutput, calls=%fused_computation.154 | convolution fusion | flops 2468608512 | bytes 34230272 | tf_op jit(solution)/shard_map/dot_general | solution.py:56
  284.9 5.7 fusion.101
  309.8 4.9 fusion.77
  335.2 161.7 %while.27 = (s32[]{:T(128)}, f32[2048,6,64]{0,2,1:T(8,128)}, f32[2048,6,64]{0,2,1:T(8,128)}, f32[4,512,6,64]{1,3,2,0:T(8,128)}, s32[4]{0:T(128)S(1)}, /*index=5*...) while((s32[]{:T(128)}, f32[2048,6,64]{0,2,1:T(8,128)}, ...), condition=%wide.region_13.14_spmd, body=%wide.region_11.13_spmd.sunk | while | flops 1546810368 | bytes 152079728 | solution.py:204
  345.7 5.4 fusion.149
  351.1 5.4 dynamic_update_slice.30
  356.5 6.6 multiply_reduce_fusion.5
  371.1 5.0 dynamic_update_slice.29
  386.5 5.4 fusion.149
  392.0 5.4 dynamic_update_slice.30
  397.3 6.6 multiply_reduce_fusion.5
  411.9 5.1 dynamic_update_slice.29
  427.4 5.4 fusion.149
  432.8 5.2 dynamic_update_slice.30
  438.0 6.6 multiply_reduce_fusion.5
  452.6 4.9 dynamic_update_slice.29
  467.9 5.4 fusion.149
  477.9 6.6 multiply_reduce_fusion.5
  507.2 4.8 fusion.75
  514.7 7.3 %fusion.100 = (f32[384]{0:T(512)S(1)}, f32[2048,384]{1,0:T(8,128)}) fusion(bf16[384,1152]{1,0:T(8,128)(2,1)} %copy-done.25, bf16[2048,384]{0,1:T(8,128)(2,1)} %bitcast.126, bf16[2048,384]{0,1:T(8,128)(2,1)} %bitcast.124, bf16[2048,384]{0,1:T(8,128)(2,1)S(1)} %bitcast.122), kind=kOutput, calls=%fused_computation.152 | convolution fusion | flops 1826881152 | bytes 8750592 | tf_op jit(solution)/shard_map/dot_general | solution.py:56
  533.4 37.6 %all-reduce.5 = f32[4608]{0:T(1024)S(1)} all-reduce(f32[4608]{0:T(1024)S(1)} %constant_dynamic-update-slice_fusion), channel_id=6, replica_groups=mesh['dp'=8,'fsdp'=4] {'dp','fsdp'}, use_global_device_ids=true, to_apply=%region_29.30.clone | all-reduce | flops 4608 | bytes 36864
  571.6 104.2 %all-reduce.9.cloned.1.call-done = (f32[442368]{0:T(1024)}, f32[147456]{0:T(1024)}, f32[589824]{0:T(1024)}, f32[589824]{0:T(1024)}) async-done(((f32[442368]{0:T(1024)}, f32[147456]{0:T(1024)}, f32[589824]{0:T(1024)}, f32[589824]{0:T(1024)}), (f32[442368]{0:T(1024)}, f32[147456]{0:T(1024)}, f32[589824]{0:T(1024)}, f32[589824]{0:T(1024)})) %all-reduce.9.cloned.1.call-update) | async-done | bytes 7077904
  (295 shorter events, 210.7 us)
Async XLA Ops:
  7.2 94.9 %copy-start.19 = (bf16[2048,384]{1,0:T(8,128)(2,1)S(1)}, bf16[2048,384]{1,0:T(8,128)(2,1)}, u32[]{:S(2)}) copy-start(bf16[2048,384]{1,0:T(8,128)(2,1)} %param.13) | copy-start | bytes 4718596
  7.2 220.5 %all-gather.5.cloned.1.call-start = ((), (), s32[]{:S(2)}) async-start(), calls=%async_computation | async-start | bytes 1216512 | tf_op jit(solution)/shard_map/all_gather | solution.py:81
  7.9 258.0 %all-gather.7.cloned.1.call-start = ((), (), s32[]{:S(2)}) async-start(), calls=%async_computation.1 | async-start | bytes 1216512 | tf_op jit(solution)/shard_map/all_gather | solution.py:82
  8.7 667.1 %all-reduce.9.cloned.1.call-start = ((), (), s32[]{:S(2)}) async-start(), calls=%async_computation.2 | async-start | bytes 14155776
  52.5 105.1 %copy-start.36 = (f32[384]{0:T(512)}, f32[384]{0:T(512)S(1)}, u32[]{:S(2)}) copy-start(f32[384]{0:T(512)S(1)} %get-tuple-element.279) | copy-start | bytes 4612
  52.5 105.1 %copy-start.43 = (f32[384]{0:T(512)}, f32[384]{0:T(512)S(1)}, u32[]{:S(2)}) copy-start(f32[384]{0:T(512)S(1)} %get-tuple-element.280) | copy-start | bytes 4612
  102.9 54.7 %copy-start.1 = (bf16[2048,384]{0,1:T(8,128)(2,1)}, bf16[2048,384]{0,1:T(8,128)(2,1)S(1)}, u32[]{:S(2)}) copy-start(bf16[2048,384]{0,1:T(8,128)(2,1)S(1)} %copy.43) | copy-start | bytes 4718596
  103.1 54.5 %copy-start.28 = (f32[2048]{0:T(1024)}, f32[2048]{0:T(1024)S(1)}, u32[]{:S(2)}) copy-start(f32[2048]{0:T(1024)S(1)} %broadcast_multiply_fusion.1) | copy-start | bytes 24580
  104.9 52.8 %copy-start.33 = (f32[2048]{0:T(1024)}, f32[2048]{0:T(1024)S(1)}, u32[]{:S(2)}) copy-start(f32[2048]{0:T(1024)S(1)} %fusion.85) | copy-start | bytes 24580
  221.7 4.3 copy-start.4
  221.7 4.3 copy-start.11
  221.7 4.3 copy-start.2
  221.7 4.3 copy-start.17
  231.1 38.2 %copy-start.35 = (f32[2048]{0:T(1024)S(1)}, f32[2048]{0:T(1024)}, u32[]{:S(2)}) copy-start(f32[2048]{0:T(1024)} %fusion.84) | copy-start | bytes 24580
  269.3 15.5 %copy-start.24 = (bf16[384,1536]{1,0:T(8,128)(2,1)S(1)}, bf16[384,1536]{1,0:T(8,128)(2,1)}, u32[]{:S(2)}) copy-start(bf16[384,1536]{1,0:T(8,128)(2,1)} %reshape.232) | copy-start | bytes 3538948
  301.2 8.5 %slice-start.3 = ((s8[6291456]{0:T(1024)(128)(4,1)}), s8[4194304]{0:T(1024)(128)(4,1)S(1)}, s32[]{:S(2)}) async-start(s8[6291456]{0:T(1024)(128)(4,1)} %bitcast.129), calls=%async_computation.6 | async-start | bytes 8388608
  303.2 6.6 slice-start.4
  309.8 4.9 copy-start.23
  309.8 4.9 copy-start.45
  321.8 4.8 copy-start.18
  351.1 12.0 %slice-start = ((s8[9437184]{0:T(1024)(128)(4,1)}), s8[1048576]{0:T(1024)(128)(4,1)S(1)}, s32[]{:S(2)}) async-start(s8[9437184]{0:T(1024)(128)(4,1)} %bitcast.113), calls=%async_computation.3 | async-start | bytes 2097152 | tf_op jit(solution)/shard_map/while
  356.5 6.7 slice-start.1
  356.5 6.7 slice-start.2
  392.0 12.0 %slice-start = ((s8[9437184]{0:T(1024)(128)(4,1)}), s8[1048576]{0:T(1024)(128)(4,1)S(1)}, s32[]{:S(2)}) async-start(s8[9437184]{0:T(1024)(128)(4,1)} %bitcast.113), calls=%async_computation.3 | async-start | bytes 2097152 | tf_op jit(solution)/shard_map/while
  397.3 6.7 slice-start.1
  397.3 6.7 slice-start.2
  432.8 11.8 %slice-start = ((s8[9437184]{0:T(1024)(128)(4,1)}), s8[1048576]{0:T(1024)(128)(4,1)S(1)}, s32[]{:S(2)}) async-start(s8[9437184]{0:T(1024)(128)(4,1)} %bitcast.113), calls=%async_computation.3 | async-start | bytes 2097152 | tf_op jit(solution)/shard_map/while
  438.0 6.7 slice-start.1
  438.0 6.7 slice-start.2
  473.2 11.3 %slice-start = ((s8[9437184]{0:T(1024)(128)(4,1)}), s8[1048576]{0:T(1024)(128)(4,1)S(1)}, s32[]{:S(2)}) async-start(s8[9437184]{0:T(1024)(128)(4,1)} %bitcast.113), calls=%async_computation.3 | async-start | bytes 2097152 | tf_op jit(solution)/shard_map/while
  477.9 6.6 slice-start.1
  477.9 6.6 slice-start.2
  (37 other events, 95.1 us)
Sparse Core Ops, SparseCore 0:
  10.9 56.7 all-gather.4
  70.5 53.3 all-gather.6
  513.5 162.2 all-reduce.8
where the time goes:
time: 700 us; the launch traced here: 689 us
  matrix products  197 us (28%)
  blocking collectives  164 us (23%)
  local copies, waits for them, and re-layouts  133 us (19%)
  waiting for transfers between devices  106 us (15%)
  other arithmetic  57.8 us (8%)
  loops' own time  16.4 us (2%)
  between operations  14.8 us (2%)
    unnamed x4, waiting for transfers between devices  106 us
    unnamed x2, blocking collectives  79.8 us
    dot_general x4, matrix products, matmul_low(): return jnp.dot(left_side, right_side, preferred_element_type=jnp.float32)  42.6 us
    all_gather x1, blocking collectives, local(): lax.all_gather(w_qkv, ('dp', 'fsdp'), axis=0, tiled=True)  42.1 us
    all_gather x1, blocking collectives, local(): lax.all_gather(w_out, ('dp', 'fsdp'), axis=0, tiled=True)  42.1 us
    dynamic_update_slice x8, local copies, waits for them, and re-layouts, add_window(): lax.dynamic_update_slice_in_dim(total, current + part_sum, window_start, 0)  39.8 us
    dot_general x4, matrix products, contract_cols(): lax.dot_general(left_side, right_side, (((1,), (1,)), ((), ())), preferre...  30.8 us
    dot_general x4, matrix products, attend_back(): jnp.einsum('qhd,khd->hqk', upstream_block, value_window, preferred_elemen...  26.5 us
  transfers between devices with their start and end apart: 3, of which 1 were waited for; matrix products, arithmetic and copies ran while one was open for 20% of the time, Pallas kernels for 0%

commit v1 on v0

v1 whole, which is shorter than its diff:
```python
import functools

import jax
import jax.numpy as jnp
from jax import lax
from jax.experimental import pallas as pl
from jax.experimental.pallas import tpu as pltpu
from jax.sharding import PartitionSpec as P

HEADS = 6
HEAD_DIM = 64
FF = 1536
D = HEADS * HEAD_DIM
PAIRS = D // 128
MAX_IMG = 66
NORM_EPS = 1e-06
MASKED = -1e30
F32 = jnp.float32
BF16 = jnp.bfloat16

GAIN1, GAIN2, BIAS1, BIAS2, BQ, BV, BOUT, BDOWN, BUP = range(9)
SMALL_ROWS = 16

TQ = 128
MARGIN = 16 * ((MAX_IMG - 1 + 15) // 16)
WIN = TQ + 2 * MARGIN


def nn(a, b):
    return jnp.dot(a, b, preferred_element_type=F32)


def nt(a, b):
    return lax.dot_general(a, b, (((1,), (1,)), ((), ())), preferred_element_type=F32)


def tn(a, b):
    return lax.dot_general(a, b, (((0,), (0,)), ((), ())), preferred_element_type=F32)


def normalize(x):
    center = jnp.mean(x, axis=-1, keepdims=True)
    off = x - center
    r = lax.rsqrt(jnp.mean(off * off, axis=-1, keepdims=True) + NORM_EPS)
    return off * r, r


def norm_back(grad, gain, xhat, r):
    gx = grad * gain
    return r * (gx - jnp.mean(gx, axis=-1, keepdims=True) - xhat * jnp.mean(gx * xhat, axis=-1, keepdims=True))


def colsum(x):
    return jnp.sum(x, axis=0, keepdims=True)


def gelu_parts(u):
    e = jnp.exp(u * u * -0.5)
    t = 1.0 / (1.0 + jnp.abs(u) * (0.3275911 * 0.7071067811865476))
    poly = t * (0.127414796 + t * (-0.142248368 + t * (0.7107068705 + t * (-0.7265760135 + t * 0.5307027145))))
    tail = poly * e
    cdf = jnp.where(u >= 0.0, 1.0 - tail, tail)
    return cdf, e * 0.3989422804014327


def half_masks(rows):
    lane = lax.broadcasted_iota(jnp.int32, (rows, 128), 1)
    low = (lane < HEAD_DIM).astype(F32).astype(BF16)
    return low, (1.0 - low.astype(F32)).astype(BF16)


def stack_heads(x, masks):
    return jnp.concatenate([x * masks[0], x * masks[1]], axis=0)


def compute(tok, cot, lens, segr, wqkv, wout, wup, wdown, small, out, ingrad, gqkv, gout, gup, gdown, gsmall,
            normed, qkv, attn, mgrad, dq, dk, dv, lse, segc, act, ul):
    rows_count = tok.shape[0]
    tiles = rows_count // TQ

    def srow(i):
        return small[i : i + 1, :]

    total = jnp.sum(lens[...], axis=-1, keepdims=True)

    R1 = 256

    def p1(i, c):
        rows = pl.ds(pl.multiple_of(i * R1, R1), R1)
        xhat, _ = normalize(tok[rows, :].astype(F32))
        n = (xhat * srow(GAIN1) + srow(BIAS1)).astype(BF16)
        normed[rows, :] = n
        qkv[rows, 0:D] = (nn(n, wqkv[:, 0:D]) + srow(BQ)).astype(BF16) * jnp.asarray(HEAD_DIM ** -0.5, BF16)
        qkv[rows, D : 2 * D] = nn(n, wqkv[:, D : 2 * D]).astype(BF16)
        qkv[rows, 2 * D : 3 * D] = (nn(n, wqkv[:, 2 * D : 3 * D]) + srow(BV)).astype(BF16)
        return c

    lax.fori_loop(0, rows_count // R1, p1, 0)

    def pseg(i, c):
        rows = pl.ds(pl.multiple_of(i * 128, 128), 128)
        segc[rows, :] = jnp.broadcast_to(segr[pl.ds(i, 1), :], (128, 128)).T
        return c

    lax.fori_loop(0, rows_count // 128, pseg, 0)

    masks = half_masks(TQ)

    def window(i):
        b = pl.multiple_of(i * TQ, TQ)
        ws = jnp.clip(b - MARGIN, 0, rows_count - WIN)
        return pl.ds(b, TQ), pl.ds(pl.multiple_of(ws, 16), WIN)

    def allowed(i, wrows):
        segk = segc[wrows, :]
        segq = jnp.broadcast_to(segr[pl.ds(i, 1), :], (WIN, 128))
        return jnp.concatenate([segk, segk], axis=1) == jnp.concatenate([segq, segq], axis=1)

    def unstack_t(x):
        return jnp.concatenate([x[:HEAD_DIM, :TQ], x[HEAD_DIM:, TQ:]], axis=0).T

    def p2(i, c):
        qrows, wrows = window(i)
        mask = allowed(i, wrows)
        for j in range(PAIRS):
            q2 = stack_heads(qkv[qrows, j * 128 : (j + 1) * 128], masks)
            kw = qkv[wrows, D + j * 128 : D + (j + 1) * 128]
            vw = qkv[wrows, 2 * D + j * 128 : 2 * D + (j + 1) * 128]
            s = jnp.where(mask, nt(kw, q2), MASKED)
            m = jnp.max(s, axis=0, keepdims=True)
            e = jnp.exp(s - m)
            l = jnp.sum(e, axis=0, keepdims=True)
            o = tn(vw, e.astype(BF16)) * (1.0 / l)
            attn[qrows, j * 128 : (j + 1) * 128] = unstack_t(o).astype(BF16)
            lse[pl.ds(i * PAIRS + j, 1), :] = m + jnp.log(l)
        return c

    lax.fori_loop(0, tiles, p2, 0)

    gout[...] = jnp.zeros_like(gout)
    gup[...] = jnp.zeros_like(gup)
    gdown[...] = jnp.zeros_like(gdown)
    gqkv[...] = jnp.zeros_like(gqkv)
    gsmall[...] = jnp.zeros_like(gsmall)
    dk[...] = jnp.zeros_like(dk)
    dv[...] = jnp.zeros_like(dv)
    R3 = act.shape[0]
    CH = 384

    def p3(i, c):
        r0 = pl.multiple_of(i * R3, R3)
        rows = pl.ds(r0, R3)
        filled = (lax.broadcasted_iota(jnp.int32, (R3, 1), 0) + r0 < total).astype(F32)
        att = attn[rows, :]
        mixed = tok[rows, :].astype(F32) + nn(att, wout[...]) + srow(BOUT)
        xhat, r = normalize(mixed)
        n2 = (xhat * srow(GAIN2) + srow(BIAS2)).astype(BF16)
        upstream = cot[rows, :].astype(F32) * filled
        up_low = upstream.astype(BF16)
        for cidx in range(FF // CH):
            cols = slice(cidx * CH, (cidx + 1) * CH)
            u = nn(n2, wup[:, cols]) + srow(BUP + cidx)
            cdf, pdf = gelu_parts(u)
            act[:, cols] = (u * cdf).astype(BF16)
            ug = nt(up_low, wdown[cols, :]) * (cdf + u * pdf)
            gsmall[BUP + cidx : BUP + cidx + 1, :] += colsum(ug)
            ul[:, cols] = ug.astype(BF16)
        res = mixed + nn(act[...], wdown[...]) + srow(BDOWN)
        out[rows, :] = (res * filled).astype(BF16)
        ng = nt(ul[...], wup[...])
        mg = upstream + norm_back(ng, srow(GAIN2), xhat, r)
        gsmall[GAIN2 : GAIN2 + 1, :] += colsum(ng * xhat)
        gsmall[BIAS2 : BIAS2 + 1, :] += colsum(ng)
        gsmall[BOUT : BOUT + 1, :] += colsum(mg)
        gsmall[BDOWN : BDOWN + 1, :] += colsum(upstream)
        mgrad[rows, :] = mg
        ml = mg.astype(BF16)
        gout[...] += tn(att, ml)
        attn[rows, :] = nt(ml, wout[...]).astype(BF16)
        for cidx in range(FF // CH):
            cols = slice(cidx * CH, (cidx + 1) * CH)
            gdown[cols, :] += tn(act[:, cols], up_low)
            gup[:, cols] += tn(n2, ul[:, cols])
        return c

    lax.fori_loop(0, rows_count // R3, p3, 0)

    def p4(i, c):
        qrows, wrows = window(i)
        mask = allowed(i, wrows)
        for j in range(PAIRS):
            cols = slice(j * 128, (j + 1) * 128)
            q2 = stack_heads(qkv[qrows, cols], masks)
            do2 = stack_heads(attn[qrows, cols], masks)
            kw = qkv[wrows, D + j * 128 : D + (j + 1) * 128]
            vw = qkv[wrows, 2 * D + j * 128 : 2 * D + (j + 1) * 128]
            s = jnp.where(mask, nt(kw, q2), MASKED)
            p = jnp.exp(s - lse[pl.ds(i * PAIRS + j, 1), :])
            dp = nt(vw, do2)
            delta = jnp.sum(p * dp, axis=0, keepdims=True)
            ds = (p * (dp - delta)).astype(BF16)
            dv[wrows, cols] += nn(p.astype(BF16), do2)
            dk[wrows, cols] += nn(ds, q2)
            dqj = unstack_t(tn(kw, ds)) * (HEAD_DIM ** -0.5)
            gsmall[BQ : BQ + 1, cols] += colsum(dqj)
            dq[qrows, cols] = dqj.astype(BF16)
        return c

    lax.fori_loop(0, tiles, p4, 0)

    R5 = 256

    def p5(i, c):
        rows = pl.ds(pl.multiple_of(i * R5, R5), R5)
        dvr = dv[rows, :]
        gsmall[BV : BV + 1, :] += colsum(dvr)
        dproj = jnp.concatenate([dq[rows, :], dk[rows, :].astype(BF16), dvr.astype(BF16)], axis=1)
        ng = nt(dproj, wqkv[...])
        xhat, r = normalize(tok[rows, :].astype(F32))
        gsmall[GAIN1 : GAIN1 + 1, :] += colsum(ng * xhat)
        gsmall[BIAS1 : BIAS1 + 1, :] += colsum(ng)
        ingrad[rows, :] = (mgrad[rows, :] + norm_back(ng, srow(GAIN1), xhat, r)).astype(BF16)
        n = normed[rows, :]
        for cidx in range(3):
            cols = slice(cidx * D, (cidx + 1) * D)
            gqkv[:, cols] += tn(n, dproj[:, cols])
        return c

    lax.fori_loop(0, rows_count // R5, p5, 0)


def run_compute(tok, cot, lens, segr, wqkv, wout, wup, wdown, small):
    rows = tok.shape[0]
    sds = jax.ShapeDtypeStruct
    vm = pl.BlockSpec(memory_space=pltpu.VMEM)
    return pl.pallas_call(
        compute,
        out_shape=(
            sds((rows, D), BF16), sds((rows, D), BF16), sds((D, 3 * D), F32), sds((D, D), F32),
            sds((D, FF), F32), sds((FF, D), F32), sds((SMALL_ROWS, D), F32),
        ),
        in_specs=[vm] * 9,
        out_specs=(vm,) * 7,
        scratch_shapes=[
            pltpu.VMEM((rows, D), BF16),
            pltpu.VMEM((rows, 3 * D), BF16),
            pltpu.VMEM((rows, D), BF16),
            pltpu.VMEM((rows, D), F32),
            pltpu.VMEM((rows, D), BF16),
            pltpu.VMEM((rows, D), F32),
            pltpu.VMEM((rows, D), F32),
            pltpu.VMEM((rows // TQ * PAIRS, 2 * TQ), F32),
            pltpu.VMEM((rows, 128), jnp.int32),
            pltpu.VMEM((256, FF), BF16),
            pltpu.VMEM((256, FF), BF16),
        ],
        compiler_params=pltpu.CompilerParams(vmem_limit_bytes=62 << 20),
        name="layer",
    )(tok, cot, lens, segr, wqkv, wout, wup, wdown, small)


def local(tokens, cotangent, image_lengths, segment_ids, w_qkv, w_out, w_up, w_down, small_params):
    axes = ("dp", "fsdp")
    gather = lambda w: lax.all_gather(w, axes, axis=0, tiled=True)
    scatter = lambda g: lax.psum_scatter(g, axes, scatter_dimension=0, tiled=True)
    wqkv = gather(w_qkv).reshape(D, 3 * D)
    wout = gather(w_out).reshape(D, D)
    wup = gather(w_up).reshape(D, FF)
    wdown = gather(w_down).reshape(FF, D)
    small = jnp.pad(gather(small_params).astype(F32).reshape(-1, D), ((0, SMALL_ROWS - 12), (0, 0)))
    out, ingrad, gqkv, gout, gup, gdown, gsmall = run_compute(
        tokens, cotangent, image_lengths, segment_ids.reshape(-1, 128), wqkv, wout, wup, wdown, small
    )
    return (
        out, ingrad, scatter(gqkv.reshape(-1)), scatter(gout.reshape(-1)), scatter(gup.reshape(-1)),
        scatter(gdown.reshape(-1)), scatter(gsmall[:12].reshape(-1)),
    )


def solution(mesh):
    both = P(("dp", "fsdp"))
    rows = P(("dp", "fsdp"), None)
    return jax.shard_map(
        local, mesh=mesh,
        in_specs=(rows, rows, rows) + (both,) * 6,
        out_specs=(rows, rows) + (both,) * 5,
        check_vma=False,
    )
```

time: 700 us -> 439 us (0.63); the launches traced: 689 us -> 438 us
  matrix products: 197 us -> 0 us
  local copies, waits for them, and re-layouts: 133 us -> 29.1 us
  Pallas kernels: 0 us -> 97.1 us
  other arithmetic: 57.8 us -> 7.66 us
  waiting for transfers between devices: 106 us -> 124 us
  loops' own time: 16.4 us -> 0 us
    dot_general x40 -> x0, matrix products: 197 us -> none  [the longest x4 42.6 us: matmul_low(): return jnp.dot(left_side, right_side, preferred_element_type=jnp.float32)]
    pallas_call x0 -> x1, Pallas kernels: none -> 97.1 us  [run_compute(): pl.pallas_call(compute, out_shape=(sds((rows, D), BF16), sds((rows, D), B...]
    dynamic_update_slice x8 -> x0, local copies, waits for them, and re-layouts: 39.8 us -> none  [add_window(): lax.dynamic_update_slice_in_dim(total, current + part_sum, window_start, 0)]
    reduce_sum x15 -> x0, other arithmetic: 27.6 us -> none  [the longest x4 9.68 us: attend(): denominator = jnp.sum(exponent, axis=-1, keepdims=True)]
    while x35 -> x0, local copies, waits for them, and re-layouts: 21.6 us -> none
    unnamed x4, waiting for transfers between devices: 106 us -> 124 us
    another operation x2 -> x0, loops' own time: 16.4 us -> none  [the longest x1 8.31 us: local(): lax.scan(attend_back, (empty_grad, empty_grad), (query_blocks, segment_bl...]
    convert_element_type x7 -> x0, other arithmetic: 16 us -> none  [the longest x4 11.9 us: attend_back(): scores_low = scores_grad.astype(jnp.bfloat16)]
  transfers between devices with their start and end apart: 3 -> 3, of which waited for: 1 -> 1; matrix products, arithmetic and copies ran while one was open for 20% -> 4% of each run, Pallas kernels for 0% -> 0%
where the time goes in v1:
time: 439 us; the launch traced here: 438 us
  blocking collectives  166 us (38%)
  waiting for transfers between devices  124 us (28%)
  Pallas kernels  97.1 us (22%)
  local copies, waits for them, and re-layouts  29.1 us (7%)
  between operations  13.8 us (3%)
  other arithmetic  7.66 us (2%)
    unnamed x4, waiting for transfers between devices  124 us
    pallas_call x1, Pallas kernels, run_compute(): pl.pallas_call(compute, out_shape=(sds((rows, D), BF16), sds((rows, D), B...  97.1 us
    all_gather x2, blocking collectives, local(): gather = lambda w: lax.all_gather(w, axes, axis=0, tiled=True)  84.2 us
    unnamed x2, blocking collectives  81.4 us
    unnamed x13, local copies, waits for them, and re-layouts  9.7 us
  transfers between devices with their start and end apart: 3, of which 1 were waited for; matrix products, arithmetic and copies ran while one was open for 4% of the time, Pallas kernels for 0%

profile of v1, /device:TPU:0, one launch (start us, length us, event | category | flops | bytes accessed | tf_op | source)
XLA Modules:
  0.0 437.9 jit_solution(15675899131935896095)
XLA Ops:
  7.2 0.0 all-gather.5.cloned.1.call-start
  7.2 0.7 all-gather.5.cloned.1.call-update
  7.9 0.0 all-gather.7.cloned.1.call-start
  7.9 0.7 all-gather.7.cloned.1.call-update
  8.6 0.0 all-reduce.10.cloned.1.call-start
  8.7 0.9 dynamic-update-slice
  9.6 42.3 %all-reduce.1 = bf16[4608]{0:T(1024)(128)(2,1)S(1)} all-reduce(bf16[4608]{0:T(1024)(128)(2,1)S(1)} %dynamic-update-slice), channel_id=1, replica_groups=mesh['dp'=8,'fsdp'=4] {'dp','fsdp'}, use_global_device_ids=true, to_apply=%add.1 | all-reduce | flops 4608 | bytes 18432
  51.9 0.7 reshape.63
  52.6 0.8 reshape.61
  53.4 42.1 %all-gather.1 = bf16[32,1,4608]{2,1,0:T(2,128)(2,1)S(1)} all-gather(bf16[1,1,4608]{2,1,0:T(2,128)(2,1)S(1)} %reshape.63), channel_id=1, replica_groups=mesh['dp'=8,'fsdp'=4] {'dp','fsdp'}, dimensions={0}, use_global_device_ids=true | all-gather | bytes 304128 | tf_op jit(solution)/shard_map/all_gather | solution.py:264
  95.4 1.7 reduce.1
  97.2 1.1 reshape.50.wout
  98.2 42.2 %all-gather = bf16[32,1,13824]{2,1,0:T(2,128)(2,1)S(1)} all-gather(bf16[1,1,13824]{2,1,0:T(2,128)(2,1)S(1)} %reshape.61), channel_id=1, replica_groups=mesh['dp'=8,'fsdp'=4] {'dp','fsdp'}, dimensions={0}, use_global_device_ids=true | all-gather | bytes 912384 | tf_op jit(solution)/shard_map/all_gather | solution.py:264
  140.4 5.3 %reduce = bf16[32,13824]{1,0:T(8,128)(2,1)S(1)} reduce(bf16[32,1,13824]{2,1,0:T(2,128)(2,1)S(1)} %all-gather, bf16[]{:T(256)} %constant.27), dimensions={1}, to_apply=%all-gather.reduce_sub_computation | reduce | bytes 1769474 | tf_op jit(solution)/shard_map/all_gather | solution.py:264
  145.8 2.4 reshape.49.wqkv
  148.1 0.6 pad_convert_fusion.small
  148.7 3.5 reshape.51.wup
  152.2 3.1 reshape.52.wdown
  155.3 97.1 %layer.1 = (bf16[2048,384]{1,0:T(8,128)(2,1)}, bf16[2048,384]{1,0:T(8,128)(2,1)}, f32[384,1152]{1,0:T(8,128)}, f32[384,384]{1,0:T(8,128)}, f32[384,1536]{1,0:T(8...) custom-call(bf16[2048,384]{1,0:T(8,128)(2,1)} %tok.1, bf16[2048,384]{1,0:T(8,128)(2,1)} %cot.1, s32[1,112]{1,0:T(1,128)} %lens.1, ...), custom_call_target="tpu_custom_call" | custom-call | tf_op jit(solution)/shard_map/layer/pallas_call | solution.py:236
  252.3 2.0 reshape.55
  254.3 2.5 reshape.54
  256.8 3.3 reshape.56
  260.1 1.6 reshape.57
  261.8 0.0 all-reduce.10.cloned.1.call-update
  261.8 0.7 copy-done.1
  262.5 39.1 %all-reduce.6 = f32[4608]{0:T(1024)S(1)} all-reduce(f32[4608]{0:T(1024)S(1)} %reshape.58), channel_id=6, replica_groups=mesh['dp'=8,'fsdp'=4] {'dp','fsdp'}, use_global_device_ids=true, to_apply=%region_4.5.clone | all-reduce | flops 4608 | bytes 36864
  301.6 0.6 dynamic-slice.4
  302.3 123.1 %all-reduce.10.cloned.1.call-done = (f32[442368]{0:T(1024)}, f32[147456]{0:T(1024)}, f32[589824]{0:T(1024)}, f32[589824]{0:T(1024)}) async-done(((f32[442368]{0:T(1024)}, f32[147456]{0:T(1024)}, f32[589824]{0:T(1024)}, f32[589824]{0:T(1024)}), (f32[442368]{0:T(1024)}, f32[147456]{0:T(1024)}, f32[589824]{0:T(1024)}, f32[589824]{0:T(1024)})) %all-reduce.10.cloned.1.call-update) | async-done | bytes 7077904
  425.3 1.5 dynamic-slice.2
  426.9 1.5 dynamic-slice.3
  428.4 1.5 dynamic-slice
  429.9 1.4 dynamic-slice.1
  (8 shorter events, 0.0 us)
Async XLA Ops:
  7.2 141.6 %all-gather.5.cloned.1.call-start = ((), (), s32[]{:S(2)}) async-start(), calls=%async_computation | async-start | bytes 1216512 | tf_op jit(solution)/shard_map/all_gather | solution.py:264
  7.9 144.3 %all-gather.7.cloned.1.call-start = ((), (), s32[]{:S(2)}) async-start(), calls=%async_computation.1 | async-start | bytes 1216512 | tf_op jit(solution)/shard_map/all_gather | solution.py:264
  8.6 416.7 %all-reduce.10.cloned.1.call-start = ((), (), s32[]{:S(2)}) async-start(), calls=%async_computation.2 | async-start | bytes 14155776
  256.8 3.3 copy-start
  261.8 0.7 copy-start.1
Sparse Core Ops, SparseCore 0:
  10.9 56.9 all-gather.4
  70.8 55.0 all-gather.6
  261.9 163.3 all-reduce.9

commit v2 on v1

--- a/solution.py
+++ b/solution.py
@@ -259,6 +259,410 @@
     )(tok, cot, lens, segr, wqkv, wout, wup, wdown, small)
 
 
+BLOCK = 160
+ROWS_A = slice(0, 64)
+ROWS_B = slice(64, 160)
+NSEM = 11
+
+
+class Place:
+    def __init__(self):
+        dp, f = lax.axis_index("dp"), lax.axis_index("fsdp")
+        self.z, self.y = lax.div(dp, 2), lax.rem(dp, 2)
+        self.x, self.c = lax.div(f, 2), lax.rem(f, 2)
+        self.dp, self.f = dp, f
+        self.ypeer = (self.z * 2 + 1 - self.y, f)
+        self.xpeer = (dp, (1 - self.x) * 2 + self.c)
+        self.cpeer = (dp, self.x * 2 + 1 - self.c)
+
+    def zpeer(self, k):
+        return (lax.rem(self.z + k, 4) * 2 + self.y, self.f)
+
+    def peers(self):
+        return [self.ypeer, self.xpeer, self.cpeer] + [self.zpeer(k) for k in (1, 2, 3)]
+
+
+def greet(at):
+    barrier = pltpu.get_barrier_semaphore()
+    for peer in at.peers():
+        pl.semaphore_signal(barrier, inc=1, device_id=peer, device_id_type=pl.DeviceIdType.MESH)
+    pl.semaphore_wait(barrier, 6)
+
+
+def send(src, dst, ssem, rsem, i, peer):
+    return pltpu.make_async_remote_copy(
+        src_ref=src, dst_ref=dst, send_sem=ssem.at[i], recv_sem=rsem.at[i],
+        device_id=peer, device_id_type=pl.DeviceIdType.MESH,
+    )
+
+
+class Gather:
+    def __init__(self, buf, rows, ssem, rsem, at):
+        z, y, x, c = at.z, at.y, at.x, at.c
+        whole = slice(None)
+
+        def copy(i, peer, zs, ys, xs):
+            ref = buf.at[zs, ys, xs, c, rows]
+            return send(ref, ref, ssem, rsem, i, peer)
+
+        self.zs = [copy(k - 1, at.zpeer(k), z, y, x) for k in (1, 2, 3)]
+        self.own = [copy(3, at.ypeer, whole, y, x), copy(4, at.xpeer, whole, y, x), copy(5, at.cpeer, whole, y, x)]
+        self.relay = [
+            copy(6, at.ypeer, pl.ds(0, 2), y, 1 - x), copy(7, at.xpeer, pl.ds(2, 2), 1 - y, x),
+            copy(8, at.cpeer, whole, y, 1 - x), copy(9, at.cpeer, whole, 1 - y, x),
+        ]
+        self.last = copy(10, at.cpeer, whole, 1 - y, 1 - x)
+
+    def step0(self):
+        for s in self.zs:
+            s.start()
+
+    def step1(self):
+        for s in self.zs:
+            s.wait_recv()
+        for s in self.own:
+            s.start()
+
+    def step2(self):
+        self.own[0].wait_recv()
+        self.own[1].wait_recv()
+        for s in self.relay:
+            s.start()
+
+    def step3(self):
+        self.relay[0].wait_recv()
+        self.relay[1].wait_recv()
+        self.last.start()
+
+    def step4(self):
+        for s in (self.own[2], self.relay[2], self.relay[3], self.last):
+            s.wait_recv()
+        for s in self.zs + self.own + self.relay + [self.last]:
+            s.wait_send()
+
+
+def divide(i, by):
+    return lax.shift_right_logical(i * ((65536 + by - 1) // by), 16)
+
+
+def swap_matrix():
+    j = lax.broadcasted_iota(jnp.int32, (192, 192), 0)
+    i = lax.broadcasted_iota(jnp.int32, (192, 192), 1)
+    outer = divide(i, 48)
+    rest = i - 48 * outer
+    inner = divide(rest, 12)
+    return (j == 48 * inner + 12 * outer + (rest - 12 * inner)).astype(F32).astype(BF16)
+
+
+def onehot(cond):
+    return cond.astype(F32).astype(BF16)
+
+
+def small_maps():
+    iota = lambda shape, d: lax.broadcasted_iota(jnp.int32, shape, d)
+    q, lane = iota((96, D), 0), iota((96, D), 1)
+    chunk = divide(lane, 48)
+    third = q - 3 * divide(q, 3)
+    eighth = q - 8 * divide(q, 8)
+    m1 = onehot(chunk == third)
+    m2 = onehot(chunk == eighth)
+    e = onehot(divide(iota((96, 32), 0), 3) == iota((96, 32), 1))
+    et = onehot(divide(iota((32, 96), 1), 3) == iota((32, 96), 0))
+    a = onehot(divide(iota((SMALL_ROWS, 96), 1), 8) == iota((SMALL_ROWS, 96), 0))
+    at = onehot(divide(iota((96, SMALL_ROWS), 0), 8) == iota((96, SMALL_ROWS), 1))
+    k, l = iota((D, D), 0), iota((D, D), 1)
+    lr = onehot((k - 48 * divide(k, 48)) == (l - 48 * divide(l, 48)))
+    return m1, m2, e, et, a, at, lr
+
+
+def small_table(rows32):
+    m1, m2, e, _, a, _, lr = small_maps()
+    t = nn(e, rows32).astype(BF16) * m1
+    t = nn(t, lr).astype(BF16) * m2
+    return nn(a, t)
+
+
+def small_rows(table):
+    m1, m2, _, et, _, at, lr = small_maps()
+    t = nn(at, table).astype(BF16) * m2
+    t = nn(t, lr).astype(BF16) * m1
+    return nn(et, t).astype(BF16)
+
+
+def pack_share(block, fqkv, fout, fup, fdown, fsmall, flat, stage):
+    block[0:16, :] = fsmall[...]
+    for at, parts in ((16, ((fqkv, 9, 0), (fout, 3, 3))), (64, ((fup, 12, 0),))):
+        for ref, per, group in parts:
+            n = ref.shape[0]
+            flat[0:n, :] = ref[...].astype(F32)
+            for j in range(per):
+                g = group + j // 3
+                stage[12 * g : 12 * g + 12, (j % 3) * 128 : (j % 3 + 1) * 128] = flat[pl.ds(j, 12, stride=per), :]
+        block[at : at + 48, :] = stage[...].astype(BF16)
+    flat[...] = fdown[...].astype(F32)
+    for j in range(3):
+        block[112:160, j * 128 : (j + 1) * 128] = flat[pl.ds(j, 48, stride=3), :].astype(BF16)
+
+
+def unpack_quad(buf, p, first, swap):
+    z, y = lax.div(p, 2), lax.rem(p, 2)
+    quad = buf[z, y, :, :, first : first + 48, :].reshape(192, D)
+    return nn(swap, quad).astype(BF16)
+
+
+def unpack_a(buf, swap, wqkv, wout):
+    def body(p, carry):
+        rows = pl.ds(pl.multiple_of(p * 48, 16), 48)
+        m = unpack_quad(buf, p, 16, swap)
+        for g in range(3):
+            wqkv[rows, g * D : (g + 1) * D] = m[48 * g : 48 * g + 48]
+        wout[rows, :] = m[144:192]
+        return carry
+
+    lax.fori_loop(0, 8, body, 0)
+
+
+def unpack_b(buf, swap, wup, wdown):
+    def body(p, carry):
+        z, y = lax.div(p, 2), lax.rem(p, 2)
+        rows = pl.ds(pl.multiple_of(p * 48, 16), 48)
+        m = unpack_quad(buf, p, 64, swap)
+        for g in range(4):
+            wup[rows, g * D : (g + 1) * D] = m[48 * g : 48 * g + 48]
+        wdown[pl.ds(pl.multiple_of(p * 192, 16), 192), :] = buf[z, y, :, :, 112:160, :].reshape(192, D)
+        return carry
+
+    lax.fori_loop(0, 8, body, 0)
+
+
+def gather_kernel(fqkv, fout, fup, fdown, fsmall, wqkv, wout, wup, wdown, small, buf, flat, stage, ssem, rsem):
+    at = Place()
+    pack_share(buf.at[at.z, at.y, at.x, at.c], fqkv, fout, fup, fdown, fsmall, flat, stage)
+    greet(at)
+    ga = Gather(buf, pl.ds(0, 64), ssem.at[0], rsem.at[0], at)
+    gb = Gather(buf, pl.ds(64, 96), ssem.at[1], rsem.at[1], at)
+    swap = swap_matrix()
+    ga.step0()
+    ga.step1()
+    gb.step0()
+    ga.step2()
+    gb.step1()
+    ga.step3()
+    gb.step2()
+    ga.step4()
+    unpack_a(buf, swap, wqkv, wout)
+    small[...] = small_table(buf[:, :, :, :, 0, :].reshape(32, D))
+    gb.step3()
+    gb.step4()
+    unpack_b(buf, swap, wup, wdown)
+
+
+def run_gather(fqkv, fout, fup, fdown, fsmall):
+    sds = jax.ShapeDtypeStruct
+    vm = pl.BlockSpec(memory_space=pltpu.VMEM)
+    return pl.pallas_call(
+        gather_kernel,
+        out_shape=(
+            sds((D, 3 * D), BF16), sds((D, D), BF16), sds((D, FF), BF16), sds((FF, D), BF16), sds((SMALL_ROWS, D), F32),
+        ),
+        in_specs=[vm] * 5,
+        out_specs=(vm,) * 5,
+        scratch_shapes=[
+            pltpu.VMEM((4, 2, 2, 2, BLOCK, D), BF16),
+            pltpu.VMEM((144, 128), F32),
+            pltpu.VMEM((48, D), F32),
+            pltpu.SemaphoreType.DMA((2, NSEM)),
+            pltpu.SemaphoreType.DMA((2, NSEM)),
+        ],
+        compiler_params=pltpu.CompilerParams(vmem_limit_bytes=32 << 20, collective_id=0, has_side_effects=True),
+        name="gather_weights",
+    )(fqkv, fout, fup, fdown, fsmall)
+
+
+class Scatter:
+    def __init__(self, buf, rc, rd, rn, rz, zbuf, n, ssem, rsem, at):
+        self.__dict__.update(buf=buf, rc=rc, rd=rd, rn=rn, rz=rz, zbuf=zbuf, n=n, at=at)
+        z, y, x, c = at.z, at.y, at.x, at.c
+        lo, hi = pl.ds(0, 2), pl.ds(2, 2)
+        cp = lambda i, peer, src, dst: send(src, dst, ssem, rsem, i, peer)
+        self.core = cp(0, at.cpeer, buf.at[:, :, :, 1 - c], rc)
+        self.diag = [
+            cp(1, at.xpeer, buf.at[lo, 1 - y, 1 - x, c], rd.at[0]),
+            cp(2, at.ypeer, buf.at[hi, 1 - y, 1 - x, c], rd.at[1]),
+        ]
+        self.early = [
+            cp(3, at.ypeer, buf.at[hi, 1 - y, x, c], rn.at[0, hi]),
+            cp(4, at.xpeer, buf.at[lo, y, 1 - x, c], rn.at[1, lo]),
+        ]
+        self.late = [
+            cp(5, at.ypeer, buf.at[lo, 1 - y, x, c], rn.at[0, lo]),
+            cp(6, at.xpeer, buf.at[hi, y, 1 - x, c], rn.at[1, hi]),
+        ]
+        self.zs = [cp(6 + k, at.zpeer(k), zbuf.at[lax.rem(z + k, 4)], rz.at[k - 1]) for k in (1, 2, 3)]
+
+    def step0(self):
+        self.core.start()
+
+    def step1(self):
+        at, buf, rc = self.at, self.buf, self.rc
+        self.core.wait_recv()
+
+        def add(y, x):
+            for z in range(4):
+                buf[z, y, x, at.c] = (buf[z, y, x, at.c].astype(F32) + rc[z, y, x].astype(F32)).astype(BF16)
+
+        add(1 - at.y, 1 - at.x)
+        for s in self.diag:
+            s.start()
+        add(1 - at.y, at.x)
+        add(at.y, 1 - at.x)
+        for s in self.early:
+            s.start()
+        add(at.y, at.x)
+
+    def step2(self):
+        at, buf, rd = self.at, self.buf, self.rd
+        for s in self.diag:
+            s.wait_recv()
+        for i in range(2):
+            a, b = (i, 1 - at.y, at.x, at.c), (2 + i, at.y, 1 - at.x, at.c)
+            buf[a] = (buf[a].astype(F32) + rd[0, i].astype(F32)).astype(BF16)
+            buf[b] = (buf[b].astype(F32) + rd[1, i].astype(F32)).astype(BF16)
+        for s in self.late:
+            s.start()
+
+    def step3(self):
+        at, buf, rn, zbuf = self.at, self.buf, self.rn, self.zbuf
+        for s in self.early + self.late:
+            s.wait_recv()
+        for z in range(4):
+            mine = buf[z, at.y, at.x, at.c].astype(F32)
+            zbuf[z] = (mine + rn[0, z].astype(F32) + rn[1, z].astype(F32)).astype(BF16)
+        for s in self.zs:
+            s.start()
+
+    def step4(self):
+        rz, zbuf = self.rz, self.zbuf
+        for s in self.zs:
+            s.wait_recv()
+        total = zbuf[self.at.z].astype(F32)
+        for k in range(3):
+            total = total + rz[k].astype(F32)
+        for s in [self.core] + self.diag + self.early + self.late + self.zs:
+            s.wait_send()
+        return total
+
+
+def pack_grads_b(buf, gup, gdown, swap, first):
+    def body(p, carry):
+        z, y = lax.div(p, 2), lax.rem(p, 2)
+        rows = pl.ds(pl.multiple_of(p * 48, 16), 48)
+        quad = jnp.concatenate([gup[rows, g * D : (g + 1) * D].astype(BF16) for g in range(4)], axis=0)
+        buf[z, y, :, :, first : first + 48, :] = nn(swap, quad).astype(BF16).reshape(2, 2, 48, D)
+        down = gdown[pl.ds(pl.multiple_of(p * 192, 16), 192), :].astype(BF16)
+        buf[z, y, :, :, first + 48 : first + 96, :] = down.reshape(2, 2, 48, D)
+        return carry
+
+    lax.fori_loop(0, 8, body, 0)
+
+
+def pack_grads_a(buf, gqkv, gout, gsmall, swap):
+    rows32 = small_rows(gsmall[...].astype(BF16))
+    i = lax.broadcasted_iota(jnp.int32, (512, 32), 0)
+    d = lax.broadcasted_iota(jnp.int32, (512, 32), 1)
+    spread = nn(onehot(i == 16 * d), rows32).astype(BF16)
+    buf[:, :, :, :, 0:16, :] = spread.reshape(4, 2, 2, 2, 16, D)
+
+    def body(p, carry):
+        z, y = lax.div(p, 2), lax.rem(p, 2)
+        rows = pl.ds(pl.multiple_of(p * 48, 16), 48)
+        parts = [gqkv[rows, g * D : (g + 1) * D].astype(BF16) for g in range(3)] + [gout[rows, :].astype(BF16)]
+        buf[z, y, :, :, 16:64, :] = nn(swap, jnp.concatenate(parts, axis=0)).astype(BF16).reshape(2, 2, 48, D)
+        return carry
+
+    lax.fori_loop(0, 8, body, 0)
+
+
+def unpack_rows(total, first, per, group, ref):
+    for j in range(per):
+        g = group + j // 3
+        ref[pl.ds(j, 12, stride=per), :] = total[first + 12 * g : first + 12 * g + 12, (j % 3) * 128 : (j % 3 + 1) * 128]
+
+
+def unpack_down(total, first, ref):
+    for j in range(3):
+        ref[pl.ds(j, 48, stride=3), :] = total[first : first + 48, j * 128 : (j + 1) * 128]
+
+
+def scatter_scratch(n):
+    return [
+        pltpu.VMEM((4, 2, 2, 2, n, D), BF16),
+        pltpu.VMEM((4, 2, 2, n, D), BF16),
+        pltpu.VMEM((2, 2, n, D), BF16),
+        pltpu.VMEM((2, 4, n, D), BF16),
+        pltpu.VMEM((3, n, D), BF16),
+        pltpu.VMEM((4, n, D), BF16),
+    ]
+
+
+def scatter_kernel(gqkv, gout, gup, gdown, gsmall, oqkv, oout, oup, odown, osmall, *scratch):
+    ba, bb, (ssem, rsem) = scratch[:6], scratch[6:12], scratch[12:]
+    at = Place()
+    greet(at)
+    swap = swap_matrix()
+    sa = Scatter(*ba, 64, ssem.at[0], rsem.at[0], at)
+    sb = Scatter(*bb, 96, ssem.at[1], rsem.at[1], at)
+    pack_grads_b(bb[0], gup, gdown, swap, 0)
+    sb.step0()
+    pack_grads_a(ba[0], gqkv, gout, gsmall, swap)
+    sa.step0()
+    sb.step1()
+    sa.step1()
+    sb.step2()
+    sa.step2()
+    sb.step3()
+    sa.step3()
+    tb = sb.step4()
+    unpack_rows(tb, 0, 12, 0, oup)
+    unpack_down(tb, 48, odown)
+    ta = sa.step4()
+    unpack_rows(ta, 16, 9, 0, oqkv)
+    unpack_rows(ta, 16, 3, 3, oout)
+    osmall[...] = ta[0:8, :]
+
+
+def run_scatter(gqkv, gout, gup, gdown, gsmall):
+    sds = jax.ShapeDtypeStruct
+    vm = pl.BlockSpec(memory_space=pltpu.VMEM)
+    return pl.pallas_call(
+        scatter_kernel,
+        out_shape=(
+            sds((108, 128), F32), sds((36, 128), F32), sds((144, 128), F32), sds((144, 128), F32), sds((8, D), F32),
+        ),
+        in_specs=[vm] * 5,
+        out_specs=(vm,) * 5,
+        scratch_shapes=scatter_scratch(64) + scatter_scratch(96) + [
+            pltpu.SemaphoreType.DMA((2, NSEM)),
+            pltpu.SemaphoreType.DMA((2, NSEM)),
+        ],
+        compiler_params=pltpu.CompilerParams(vmem_limit_bytes=48 << 20, collective_id=1, has_side_effects=True),
+        name="scatter_grads",
+    )(gqkv, gout, gup, gdown, gsmall)
+
+
+def lanes(flat):
+    return flat.reshape(-1, 128)
+
+
+def local_direct(tokens, cotangent, image_lengths, segment_ids, w_qkv, w_out, w_up, w_down, small_params):
+    share = small_params.shape[0]
+    fsmall = jnp.pad(small_params.reshape(1, share), ((0, 15), (0, D - share)))
+    weights = run_gather(lanes(w_qkv), lanes(w_out), lanes(w_up), lanes(w_down), fsmall)
+    out, ingrad, *grads = run_compute(tokens, cotangent, image_lengths, segment_ids.reshape(-1, 128), *weights)
+    oqkv, oout, oup, odown, osmall = run_scatter(*grads)
+    return out, ingrad, oqkv.reshape(-1), oout.reshape(-1), oup.reshape(-1), odown.reshape(-1), osmall[0, :share]
+
+
 def local(tokens, cotangent, image_lengths, segment_ids, w_qkv, w_out, w_up, w_down, small_params):
     axes = ("dp", "fsdp")
     gather = lambda w: lax.all_gather(w, axes, axis=0, tiled=True)
@@ -280,8 +684,9 @@
 def solution(mesh):
     both = P(("dp", "fsdp"))
     rows = P(("dp", "fsdp"), None)
+    direct = dict(mesh.shape) == {"dp": 8, "fsdp": 4}
     return jax.shard_map(
-        local, mesh=mesh,
+        local_direct if direct else local, mesh=mesh,
         in_specs=(rows, rows, rows) + (both,) * 6,
         out_specs=(rows, rows) + (both,) * 5,
         check_vma=False,

time: 439 us -> 184 us (0.42)
  blocking collectives: 166 us -> 0 us
  waiting for transfers between devices: 124 us -> 0 us
  Pallas kernels: 97.1 us -> 167 us
  between operations: 13.8 us -> 0.68 us
  local copies, waits for them, and re-layouts: 29.1 us -> 16 us
  other arithmetic: 7.66 us -> 0 us
    unnamed x4 -> x0, waiting for transfers between devices: 124 us -> none
    all_gather x2 -> x0, blocking collectives: 84.2 us -> none  [local(): gather = lambda w: lax.all_gather(w, axes, axis=0, tiled=True)]
    unnamed x2 -> x0, blocking collectives: 81.4 us -> none
    pallas_call x0 -> x2, Pallas kernels: none -> 69.5 us  [the longest x1 36.2 us: run_scatter(): pl.pallas_call(scatter_kernel, out_shape=(sds((108, 128), F32), sds((36,...]
    reshape x10 -> x1, local copies, waits for them, and re-layouts: 19.4 us -> 0.66 us  [local_direct(): fsmall = jnp.pad(small_params.reshape(1, share), ((0, 15), (0, D - share)))]
    all_gather x2 -> x0, other arithmetic: 7.05 us -> none  [local(): gather = lambda w: lax.all_gather(w, axes, axis=0, tiled=True)]
    unnamed x13 -> x30, local copies, waits for them, and re-layouts: 9.7 us -> 14.8 us
  transfers between devices with their start and end apart: 3 -> 0, of which waited for: 1 -> 0; matrix products, arithmetic and copies ran while one was open for 4% -> 0% of each run, Pallas kernels for 0% -> 0%
where the time goes in v2:
time: 184 us; the launch traced here: 183 us
  Pallas kernels  167 us (91%)
  local copies, waits for them, and re-layouts  16 us (9%)
    pallas_call x1, Pallas kernels, run_compute(): pl.pallas_call(compute, out_shape=(sds((rows, D), BF16), sds((rows, D), B...  97.1 us
    pallas_call x1, Pallas kernels, run_scatter(): pl.pallas_call(scatter_kernel, out_shape=(sds((108, 128), F32), sds((36,...  36.2 us
    pallas_call x1, Pallas kernels, run_gather(): pl.pallas_call(gather_kernel, out_shape=(sds((D, 3 * D), BF16), sds((D, D...  33.3 us
    unnamed x30, local copies, waits for them, and re-layouts  14.8 us

profile of v2, /device:TPU:0, one launch (start us, length us, event | category | flops | bytes accessed | tf_op | source)
XLA Modules:
  0.0 183.3 jit_solution(16727860893218458803)
XLA Ops:
  0.6 0.7 reshape.49
  1.3 0.0 copy-start.7
  1.3 0.8 copy-done.7
  2.1 0.0 copy-start.8
  2.1 0.8 copy-done.8
  2.8 0.0 copy-start.9
  2.8 0.7 copy-done.9
  3.6 0.0 copy-start.12
  3.6 0.7 copy-done.12
  4.3 33.3 %gather_weights.1 = (bf16[384,1152]{1,0:T(8,128)(2,1)S(1)}, bf16[384,384]{1,0:T(8,128)(2,1)S(1)}, bf16[384,1536]{1,0:T(8,128)(2,1)S(1)}, bf16[1536,384]{1,0:T(8,128)(2,1)S(1)}, f32[16,384]{1,0:T(8,128)S(1)}) custom-call(bf16[108,128]{1,0:T(8,128)(2,1)S(1)} %bitcast.15, bf16[36,128]{1,0:T(8,128)(2,1)S(1)} %bitcast.17, bf16[144,128]{1,0:T(8,128)(2,1)S(1)} %bitcast.13, ...), custom_call_target="tpu_custom_call" | custom-call | tf_op jit(solution)/shard_map/gather_weights/pallas_call | solution.py:463
  37.6 0.0 copy-start.2
  37.6 1.0 copy-done.2
  38.6 0.0 copy-start.3
  38.6 1.1 copy-done.3
  39.7 0.0 copy-start.4
  39.7 0.9 copy-done.4
  40.6 0.0 copy-start.6
  40.6 0.7 copy-done.6
  41.4 0.0 copy-start.10
  41.4 0.6 copy-done.10
  42.0 97.1 %layer.1 = (bf16[2048,384]{1,0:T(8,128)(2,1)}, bf16[2048,384]{1,0:T(8,128)(2,1)}, f32[384,1152]{1,0:T(8,128)}, f32[384,384]{1,0:T(8,128)}, f32[384,1536]{1,0:T(8...) custom-call(bf16[2048,384]{1,0:T(8,128)(2,1)} %tok.1, bf16[2048,384]{1,0:T(8,128)(2,1)} %cot.1, s32[1,112]{1,0:T(1,128)} %lens.1, ...), custom_call_target="tpu_custom_call" | custom-call | tf_op jit(solution)/shard_map/layer/pallas_call | solution.py:236
  139.1 0.0 copy-start
  139.1 1.7 copy-done
  140.7 1.5 copy-done.1
  142.2 1.1 copy-done.5
  143.3 0.7 copy-done.11
  144.0 36.2 %scatter_grads.1 = (f32[108,128]{1,0:T(8,128)S(1)}, f32[36,128]{1,0:T(8,128)S(1)}, f32[144,128]{1,0:T(8,128)S(1)}, f32[144,128]{1,0:T(8,128)S(1)}, f32[8,384]{1,0:T(8,128)S(1)}) custom-call(f32[384,1152]{1,0:T(8,128)S(1)} %copy-done.1, f32[384,384]{1,0:T(8,128)S(1)} %copy-done.5, f32[384,1536]{1,0:T(8,128)S(1)} %copy-done, ...), custom_call_target="tpu_custom_call" | custom-call | tf_op jit(solution)/shard_map/scatter_grads/pallas_call | solution.py:637
  180.2 0.6 slice.3
  180.8 0.6 copy.20
  181.4 0.6 copy.21
  182.0 0.6 copy.22
  182.7 0.6 copy.23
  (4 shorter events, 0.0 us)
Async XLA Ops:
  1.3 0.8 copy-start.7
  2.1 0.8 copy-start.8
  2.8 0.7 copy-start.9
  3.6 0.7 copy-start.12
  37.6 1.0 copy-start.2
  38.6 1.1 copy-start.3
  39.7 0.9 copy-start.4
  40.6 0.7 copy-start.6
  41.4 0.6 copy-start.10
  139.1 1.7 copy-start
  140.7 1.5 copy-start.1
  142.2 1.1 copy-start.5
  143.3 0.7 copy-start.11

commit v3 on v2

--- a/solution.py
+++ b/solution.py
@@ -24,6 +24,11 @@
 TQ = 128
 MARGIN = 16 * ((MAX_IMG - 1 + 15) // 16)
 WIN = TQ + 2 * MARGIN
+R1 = 256
+R3 = 256
+R5 = 256
+CH = 384
+QSCALE = HEAD_DIM ** -0.5
 
 
 def nn(a, b):
@@ -73,190 +78,223 @@
     return jnp.concatenate([x * masks[0], x * masks[1]], axis=0)
 
 
-def compute(tok, cot, lens, segr, wqkv, wout, wup, wdown, small, out, ingrad, gqkv, gout, gup, gdown, gsmall,
-            normed, qkv, attn, mgrad, dq, dk, dv, lse, segc, act, ul):
-    rows_count = tok.shape[0]
-    tiles = rows_count // TQ
-
-    def srow(i):
-        return small[i : i + 1, :]
-
-    total = jnp.sum(lens[...], axis=-1, keepdims=True)
-
-    R1 = 256
-
-    def p1(i, c):
+class Layer:
+    def __init__(self, **refs):
+        self.__dict__.update(refs)
+        self.rows_count = self.tok.shape[0]
+        self.tiles = self.rows_count // TQ
+
+    def srow(self, i):
+        return self.small[i : i + 1, :]
+
+    def loop(self, n, body, at=()):
+        def step(i, carry):
+            body(i)
+            for k, action in at:
+                pl.when(i == k)(action)
+            return carry
+
+        lax.fori_loop(0, n, step, 0)
+
+    def norm_one(self, i):
         rows = pl.ds(pl.multiple_of(i * R1, R1), R1)
-        xhat, _ = normalize(tok[rows, :].astype(F32))
-        n = (xhat * srow(GAIN1) + srow(BIAS1)).astype(BF16)
-        normed[rows, :] = n
-        qkv[rows, 0:D] = (nn(n, wqkv[:, 0:D]) + srow(BQ)).astype(BF16) * jnp.asarray(HEAD_DIM ** -0.5, BF16)
-        qkv[rows, D : 2 * D] = nn(n, wqkv[:, D : 2 * D]).astype(BF16)
-        qkv[rows, 2 * D : 3 * D] = (nn(n, wqkv[:, 2 * D : 3 * D]) + srow(BV)).astype(BF16)
-        return c
-
-    lax.fori_loop(0, rows_count // R1, p1, 0)
-
-    def pseg(i, c):
-        rows = pl.ds(pl.multiple_of(i * 128, 128), 128)
-        segc[rows, :] = jnp.broadcast_to(segr[pl.ds(i, 1), :], (128, 128)).T
-        return c
-
-    lax.fori_loop(0, rows_count // 128, pseg, 0)
-
-    masks = half_masks(TQ)
-
-    def window(i):
-        b = pl.multiple_of(i * TQ, TQ)
-        ws = jnp.clip(b - MARGIN, 0, rows_count - WIN)
-        return pl.ds(b, TQ), pl.ds(pl.multiple_of(ws, 16), WIN)
-
-    def allowed(i, wrows):
-        segk = segc[wrows, :]
-        segq = jnp.broadcast_to(segr[pl.ds(i, 1), :], (WIN, 128))
+        self.mgrad[rows, :] = normalize(self.tok[rows, :].astype(F32))[0]
+
+    def clear(self):
+        for ref in (self.gout, self.gup, self.gdown, self.gqkv, self.gsmall):
+            ref[...] = jnp.zeros_like(ref)
+
+    def clear_rows(self, i):
+        rows = pl.ds(pl.multiple_of(i * 16, 16), 16)
+        self.dk[rows, :] = jnp.zeros((16, D), F32)
+        self.dv[rows, :] = jnp.zeros((16, D), F32)
+
+    def margins(self):
+        n = self.rows_count
+        for lo in (0, MARGIN + n):
+            self.qkv[lo : lo + MARGIN, :] = jnp.zeros((MARGIN, 3 * D), BF16)
+            self.segc[lo : lo + MARGIN, :] = jnp.full((MARGIN, 128), -1, jnp.int32)
+
+    def segments(self, i):
+        rows = pl.ds(pl.multiple_of(i * 128 + MARGIN, 16), 128)
+        self.segc[rows, :] = jnp.broadcast_to(self.segr[pl.ds(i, 1), :], (128, 128)).T
+
+    def project(self, i):
+        rows = pl.ds(pl.multiple_of(i * R1, R1), R1)
+        prow = pl.ds(pl.multiple_of(i * R1 + MARGIN, 16), R1)
+        n = (self.mgrad[rows, :] * self.srow(GAIN1) + self.srow(BIAS1)).astype(BF16)
+        self.normed[rows, :] = n
+        w, out = self.wqkv, self.qkv
+        out[prow, 0:D] = (nn(n, w[:, 0:D]) + self.srow(BQ)).astype(BF16) * jnp.asarray(QSCALE, BF16)
+        out[prow, D : 2 * D] = nn(n, w[:, D : 2 * D]).astype(BF16)
+        out[prow, 2 * D : 3 * D] = (nn(n, w[:, 2 * D : 3 * D]) + self.srow(BV)).astype(BF16)
+
+    def window(self, i):
+        b = i * TQ
+        return (
+            pl.ds(pl.multiple_of(b, TQ), TQ), pl.ds(pl.multiple_of(b + MARGIN, 16), TQ),
+            pl.ds(pl.multiple_of(b, 16), WIN),
+        )
+
+    def allowed(self, i, wrows):
+        segk = self.segc[wrows, :]
+        segq = jnp.broadcast_to(self.segr[pl.ds(i, 1), :], (WIN, 128))
         return jnp.concatenate([segk, segk], axis=1) == jnp.concatenate([segq, segq], axis=1)
 
+    @staticmethod
     def unstack_t(x):
         return jnp.concatenate([x[:HEAD_DIM, :TQ], x[HEAD_DIM:, TQ:]], axis=0).T
 
-    def p2(i, c):
-        qrows, wrows = window(i)
-        mask = allowed(i, wrows)
+    def attend(self, i):
+        masks = half_masks(TQ)
+        orows, qrows, wrows = self.window(i)
+        mask = self.allowed(i, wrows)
         for j in range(PAIRS):
-            q2 = stack_heads(qkv[qrows, j * 128 : (j + 1) * 128], masks)
-            kw = qkv[wrows, D + j * 128 : D + (j + 1) * 128]
-            vw = qkv[wrows, 2 * D + j * 128 : 2 * D + (j + 1) * 128]
+            q2 = stack_heads(self.qkv[qrows, j * 128 : (j + 1) * 128], masks)
+            kw = self.qkv[wrows, D + j * 128 : D + (j + 1) * 128]
+            vw = self.qkv[wrows, 2 * D + j * 128 : 2 * D + (j + 1) * 128]
             s = jnp.where(mask, nt(kw, q2), MASKED)
             m = jnp.max(s, axis=0, keepdims=True)
             e = jnp.exp(s - m)
             l = jnp.sum(e, axis=0, keepdims=True)
             o = tn(vw, e.astype(BF16)) * (1.0 / l)
-            attn[qrows, j * 128 : (j + 1) * 128] = unstack_t(o).astype(BF16)
-            lse[pl.ds(i * PAIRS + j, 1), :] = m + jnp.log(l)
-        return c
-
-    lax.fori_loop(0, tiles, p2, 0)
-
-    gout[...] = jnp.zeros_like(gout)
-    gup[...] = jnp.zeros_like(gup)
-    gdown[...] = jnp.zeros_like(gdown)
-    gqkv[...] = jnp.zeros_like(gqkv)
-    gsmall[...] = jnp.zeros_like(gsmall)
-    dk[...] = jnp.zeros_like(dk)
-    dv[...] = jnp.zeros_like(dv)
-    R3 = act.shape[0]
-    CH = 384
-
-    def p3(i, c):
+            self.attn[orows, j * 128 : (j + 1) * 128] = self.unstack_t(o).astype(BF16)
+            self.lse[pl.ds(i * PAIRS + j, 1), :] = m + jnp.log(l)
+
+    def feed(self, i):
+        act, ul, gsmall, wout, wup, wdown = self.act, self.ul, self.gsmall, self.wout, self.wup, self.wdown
         r0 = pl.multiple_of(i * R3, R3)
         rows = pl.ds(r0, R3)
+        total = jnp.sum(self.lens[...], axis=-1, keepdims=True)
         filled = (lax.broadcasted_iota(jnp.int32, (R3, 1), 0) + r0 < total).astype(F32)
-        att = attn[rows, :]
-        mixed = tok[rows, :].astype(F32) + nn(att, wout[...]) + srow(BOUT)
+        att = self.attn[rows, :]
+        mixed = self.tok[rows, :].astype(F32) + nn(att, wout[...]) + self.srow(BOUT)
         xhat, r = normalize(mixed)
-        n2 = (xhat * srow(GAIN2) + srow(BIAS2)).astype(BF16)
-        upstream = cot[rows, :].astype(F32) * filled
+        n2 = (xhat * self.srow(GAIN2) + self.srow(BIAS2)).astype(BF16)
+        upstream = self.cot[rows, :].astype(F32) * filled
         up_low = upstream.astype(BF16)
-        for cidx in range(FF // CH):
-            cols = slice(cidx * CH, (cidx + 1) * CH)
-            u = nn(n2, wup[:, cols]) + srow(BUP + cidx)
+        for k in range(FF // CH):
+            cols = slice(k * CH, (k + 1) * CH)
+            u = nn(n2, wup[:, cols]) + self.srow(BUP + k)
             cdf, pdf = gelu_parts(u)
             act[:, cols] = (u * cdf).astype(BF16)
             ug = nt(up_low, wdown[cols, :]) * (cdf + u * pdf)
-            gsmall[BUP + cidx : BUP + cidx + 1, :] += colsum(ug)
+            gsmall[BUP + k : BUP + k + 1, :] += colsum(ug)
             ul[:, cols] = ug.astype(BF16)
-        res = mixed + nn(act[...], wdown[...]) + srow(BDOWN)
-        out[rows, :] = (res * filled).astype(BF16)
+        res = mixed + nn(act[...], wdown[...]) + self.srow(BDOWN)
+        self.out[rows, :] = (res * filled).astype(BF16)
         ng = nt(ul[...], wup[...])
-        mg = upstream + norm_back(ng, srow(GAIN2), xhat, r)
+        mg = upstream + norm_back(ng, self.srow(GAIN2), xhat, r)
         gsmall[GAIN2 : GAIN2 + 1, :] += colsum(ng * xhat)
         gsmall[BIAS2 : BIAS2 + 1, :] += colsum(ng)
         gsmall[BOUT : BOUT + 1, :] += colsum(mg)
         gsmall[BDOWN : BDOWN + 1, :] += colsum(upstream)
-        mgrad[rows, :] = mg
+        self.mgrad[rows, :] = mg
         ml = mg.astype(BF16)
-        gout[...] += tn(att, ml)
-        attn[rows, :] = nt(ml, wout[...]).astype(BF16)
-        for cidx in range(FF // CH):
-            cols = slice(cidx * CH, (cidx + 1) * CH)
-            gdown[cols, :] += tn(act[:, cols], up_low)
-            gup[:, cols] += tn(n2, ul[:, cols])
-        return c
-
-    lax.fori_loop(0, rows_count // R3, p3, 0)
-
-    def p4(i, c):
-        qrows, wrows = window(i)
-        mask = allowed(i, wrows)
+        self.gout[...] += tn(att, ml)
+        self.attn[rows, :] = nt(ml, wout[...]).astype(BF16)
+        for k in range(FF // CH):
+            cols = slice(k * CH, (k + 1) * CH)
+            self.gdown[cols, :] += tn(act[:, cols], up_low)
+            self.gup[:, cols] += tn(n2, ul[:, cols])
+
+    def attend_back(self, i):
+        masks = half_masks(TQ)
+        orows, qrows, wrows = self.window(i)
+        mask = self.allowed(i, wrows)
         for j in range(PAIRS):
             cols = slice(j * 128, (j + 1) * 128)
-            q2 = stack_heads(qkv[qrows, cols], masks)
-            do2 = stack_heads(attn[qrows, cols], masks)
-            kw = qkv[wrows, D + j * 128 : D + (j + 1) * 128]
-            vw = qkv[wrows, 2 * D + j * 128 : 2 * D + (j + 1) * 128]
+            q2 = stack_heads(self.qkv[qrows, cols], masks)
+            do2 = stack_heads(self.attn[orows, cols], masks)
+            kw = self.qkv[wrows, D + j * 128 : D + (j + 1) * 128]
+            vw = self.qkv[wrows, 2 * D + j * 128 : 2 * D + (j + 1) * 128]
             s = jnp.where(mask, nt(kw, q2), MASKED)
-            p = jnp.exp(s - lse[pl.ds(i * PAIRS + j, 1), :])
+            p = jnp.exp(s - self.lse[pl.ds(i * PAIRS + j, 1), :])
             dp = nt(vw, do2)
             delta = jnp.sum(p * dp, axis=0, keepdims=True)
             ds = (p * (dp - delta)).astype(BF16)
-            dv[wrows, cols] += nn(p.astype(BF16), do2)
-            dk[wrows, cols] += nn(ds, q2)
-            dqj = unstack_t(tn(kw, ds)) * (HEAD_DIM ** -0.5)
-            gsmall[BQ : BQ + 1, cols] += colsum(dqj)
-            dq[qrows, cols] = dqj.astype(BF16)
-        return c
-
-    lax.fori_loop(0, tiles, p4, 0)
-
-    R5 = 256
-
-    def p5(i, c):
+            self.dv[wrows, cols] += nn(p.astype(BF16), do2)
+            self.dk[wrows, cols] += nn(ds, q2)
+            dqj = self.unstack_t(tn(kw, ds)) * QSCALE
+            self.gsmall[BQ : BQ + 1, cols] += colsum(dqj)
+            self.dq[orows, cols] = dqj.astype(BF16)
+
+    def project_grad(self, i):
         rows = pl.ds(pl.multiple_of(i * R5, R5), R5)
-        dvr = dv[rows, :]
-        gsmall[BV : BV + 1, :] += colsum(dvr)
-        dproj = jnp.concatenate([dq[rows, :], dk[rows, :].astype(BF16), dvr.astype(BF16)], axis=1)
-        ng = nt(dproj, wqkv[...])
-        xhat, r = normalize(tok[rows, :].astype(F32))
-        gsmall[GAIN1 : GAIN1 + 1, :] += colsum(ng * xhat)
-        gsmall[BIAS1 : BIAS1 + 1, :] += colsum(ng)
-        ingrad[rows, :] = (mgrad[rows, :] + norm_back(ng, srow(GAIN1), xhat, r)).astype(BF16)
-        n = normed[rows, :]
-        for cidx in range(3):
-            cols = slice(cidx * D, (cidx + 1) * D)
-            gqkv[:, cols] += tn(n, dproj[:, cols])
-        return c
-
-    lax.fori_loop(0, rows_count // R5, p5, 0)
-
-
-def run_compute(tok, cot, lens, segr, wqkv, wout, wup, wdown, small):
+        prow = pl.ds(pl.multiple_of(i * R5 + MARGIN, 16), R5)
+        dvr = self.dv[prow, :]
+        self.gsmall[BV : BV + 1, :] += colsum(dvr)
+        n = self.normed[rows, :]
+        for k, part in enumerate((self.dq[rows, :], self.dk[prow, :].astype(BF16), dvr.astype(BF16))):
+            cols = slice(k * D, (k + 1) * D)
+            self.qkv[prow, cols] = part
+            self.gqkv[:, cols] += tn(n, part)
+
+    def project_back(self, i):
+        rows = pl.ds(pl.multiple_of(i * R5, R5), R5)
+        prow = pl.ds(pl.multiple_of(i * R5 + MARGIN, 16), R5)
+        ng = nt(self.qkv[prow, :], self.wqkv[...])
+        xhat, r = normalize(self.tok[rows, :].astype(F32))
+        self.gsmall[GAIN1 : GAIN1 + 1, :] += colsum(ng * xhat)
+        self.gsmall[BIAS1 : BIAS1 + 1, :] += colsum(ng)
+        self.ingrad[rows, :] = (self.mgrad[rows, :] + norm_back(ng, self.srow(GAIN1), xhat, r)).astype(BF16)
+
+
+def layer_scratch(rows):
+    padded = rows + 2 * MARGIN
+    return dict(
+        normed=pltpu.VMEM((rows, D), BF16), qkv=pltpu.VMEM((padded, 3 * D), BF16), attn=pltpu.VMEM((rows, D), BF16),
+        mgrad=pltpu.VMEM((rows, D), F32), dq=pltpu.VMEM((rows, D), BF16), dk=pltpu.VMEM((padded, D), F32),
+        dv=pltpu.VMEM((padded, D), F32), lse=pltpu.VMEM((rows // TQ * PAIRS, 2 * TQ), F32),
+        segc=pltpu.VMEM((padded, 128), jnp.int32), act=pltpu.VMEM((R3, FF), BF16), ul=pltpu.VMEM((R3, FF), BF16),
+    )
+
+
+def named_call(body, ins, outs, scratch, **options):
+    names = list(ins) + list(outs) + list(scratch)
+
+    def kernel(*refs):
+        body(**dict(zip(names, refs)))
+
+    spec = lambda space: pl.BlockSpec(memory_space=space)
+    return pl.pallas_call(
+        kernel,
+        out_shape=tuple(jax.ShapeDtypeStruct(*shape) for shape, _ in outs.values()),
+        in_specs=[spec(space) for _, space in ins.values()],
+        out_specs=tuple(spec(space) for _, space in outs.values()),
+        scratch_shapes=list(scratch.values()),
+        **options,
+    )(*(array for array, _ in ins.values()))
+
+
+def alone(**refs):
+    layer = Layer(**refs)
+    rows = layer.rows_count
+    layer.loop(rows // R1, layer.norm_one)
+    layer.clear()
+    layer.loop((rows + 2 * MARGIN) // 16, layer.clear_rows)
+    layer.margins()
+    layer.loop(rows // 128, layer.segments)
+    layer.loop(rows // R1, layer.project)
+    layer.loop(layer.tiles, layer.attend)
+    layer.loop(rows // R3, layer.feed)
+    layer.loop(layer.tiles, layer.attend_back)
+    layer.loop(rows // R5, layer.project_grad)
+    layer.loop(rows // R5, layer.project_back)
+
+
+def run_alone(tok, cot, lens, segr, wqkv, wout, wup, wdown, small):
     rows = tok.shape[0]
-    sds = jax.ShapeDtypeStruct
-    vm = pl.BlockSpec(memory_space=pltpu.VMEM)
-    return pl.pallas_call(
-        compute,
-        out_shape=(
-            sds((rows, D), BF16), sds((rows, D), BF16), sds((D, 3 * D), F32), sds((D, D), F32),
-            sds((D, FF), F32), sds((FF, D), F32), sds((SMALL_ROWS, D), F32),
-        ),
-        in_specs=[vm] * 9,
-        out_specs=(vm,) * 7,
-        scratch_shapes=[
-            pltpu.VMEM((rows, D), BF16),
-            pltpu.VMEM((rows, 3 * D), BF16),
-            pltpu.VMEM((rows, D), BF16),
-            pltpu.VMEM((rows, D), F32),
-            pltpu.VMEM((rows, D), BF16),
-            pltpu.VMEM((rows, D), F32),
-            pltpu.VMEM((rows, D), F32),
-            pltpu.VMEM((rows // TQ * PAIRS, 2 * TQ), F32),
-            pltpu.VMEM((rows, 128), jnp.int32),
-            pltpu.VMEM((256, FF), BF16),
-            pltpu.VMEM((256, FF), BF16),
-        ],
-        compiler_params=pltpu.CompilerParams(vmem_limit_bytes=62 << 20),
-        name="layer",
-    )(tok, cot, lens, segr, wqkv, wout, wup, wdown, small)
+    vm = pltpu.VMEM
+    arrays = dict(tok=tok, cot=cot, lens=lens, segr=segr, wqkv=wqkv, wout=wout, wup=wup, wdown=wdown, small=small)
+    outs = dict(
+        out=((rows, D), BF16), ingrad=((rows, D), BF16), gqkv=((D, 3 * D), F32), gout=((D, D), F32),
+        gup=((D, FF), F32), gdown=((FF, D), F32), gsmall=((SMALL_ROWS, D), F32),
+    )
+    return named_call(
+        alone, {k: (v, vm) for k, v in arrays.items()}, {k: (v, vm) for k, v in outs.items()}, layer_scratch(rows),
+        compiler_params=pltpu.CompilerParams(vmem_limit_bytes=62 << 20), name="layer",
+    )
 
 
 BLOCK = 160
@@ -389,9 +427,8 @@
     return nn(et, t).astype(BF16)
 
 
-def pack_share(block, fqkv, fout, fup, fdown, fsmall, flat, stage):
-    block[0:16, :] = fsmall[...]
-    for at, parts in ((16, ((fqkv, 9, 0), (fout, 3, 3))), (64, ((fup, 12, 0),))):
+def pack_share(block, what, flat, stage):
+    for at, parts in what:
         for ref, per, group in parts:
             n = ref.shape[0]
             flat[0:n, :] = ref[...].astype(F32)
@@ -399,6 +436,9 @@
                 g = group + j // 3
                 stage[12 * g : 12 * g + 12, (j % 3) * 128 : (j % 3 + 1) * 128] = flat[pl.ds(j, 12, stride=per), :]
         block[at : at + 48, :] = stage[...].astype(BF16)
+
+
+def pack_down(block, fdown, flat):
     flat[...] = fdown[...].astype(F32)
     for j in range(3):
         block[112:160, j * 128 : (j + 1) * 128] = flat[pl.ds(j, 48, stride=3), :].astype(BF16)
@@ -433,50 +473,6 @@
         return carry
 
     lax.fori_loop(0, 8, body, 0)
-
-
-def gather_kernel(fqkv, fout, fup, fdown, fsmall, wqkv, wout, wup, wdown, small, buf, flat, stage, ssem, rsem):
-    at = Place()
-    pack_share(buf.at[at.z, at.y, at.x, at.c], fqkv, fout, fup, fdown, fsmall, flat, stage)
-    greet(at)
-    ga = Gather(buf, pl.ds(0, 64), ssem.at[0], rsem.at[0], at)
-    gb = Gather(buf, pl.ds(64, 96), ssem.at[1], rsem.at[1], at)
-    swap = swap_matrix()
-    ga.step0()
-    ga.step1()
-    gb.step0()
-    ga.step2()
-    gb.step1()
-    ga.step3()
-    gb.step2()
-    ga.step4()
-    unpack_a(buf, swap, wqkv, wout)
-    small[...] = small_table(buf[:, :, :, :, 0, :].reshape(32, D))
-    gb.step3()
-    gb.step4()
-    unpack_b(buf, swap, wup, wdown)
-
-
-def run_gather(fqkv, fout, fup, fdown, fsmall):
-    sds = jax.ShapeDtypeStruct
-    vm = pl.BlockSpec(memory_space=pltpu.VMEM)
-    return pl.pallas_call(
-        gather_kernel,
-        out_shape=(
-            sds((D, 3 * D), BF16), sds((D, D), BF16), sds((D, FF), BF16), sds((FF, D), BF16), sds((SMALL_ROWS, D), F32),
-        ),
-        in_specs=[vm] * 5,
-        out_specs=(vm,) * 5,
-        scratch_shapes=[
-            pltpu.VMEM((4, 2, 2, 2, BLOCK, D), BF16),
-            pltpu.VMEM((144, 128), F32),
-            pltpu.VMEM((48, D), F32),
-            pltpu.SemaphoreType.DMA((2, NSEM)),
-            pltpu.SemaphoreType.DMA((2, NSEM)),
-        ],
-        compiler_params=pltpu.CompilerParams(vmem_limit_bytes=32 << 20, collective_id=0, has_side_effects=True),
-        name="gather_weights",
-    )(fqkv, fout, fup, fdown, fsmall)
 
 
 class Scatter:
@@ -566,18 +562,19 @@
     lax.fori_loop(0, 8, body, 0)
 
 
-def pack_grads_a(buf, gqkv, gout, gsmall, swap):
+def pack_grads_small(buf, gsmall):
     rows32 = small_rows(gsmall[...].astype(BF16))
     i = lax.broadcasted_iota(jnp.int32, (512, 32), 0)
     d = lax.broadcasted_iota(jnp.int32, (512, 32), 1)
-    spread = nn(onehot(i == 16 * d), rows32).astype(BF16)
-    buf[:, :, :, :, 0:16, :] = spread.reshape(4, 2, 2, 2, 16, D)
-
+    buf[...] = nn(onehot(i == 16 * d), rows32).astype(BF16).reshape(4, 2, 2, 2, 16, D)
+
+
+def pack_grads_a(buf, gqkv, gout, swap):
     def body(p, carry):
         z, y = lax.div(p, 2), lax.rem(p, 2)
         rows = pl.ds(pl.multiple_of(p * 48, 16), 48)
         parts = [gqkv[rows, g * D : (g + 1) * D].astype(BF16) for g in range(3)] + [gout[rows, :].astype(BF16)]
-        buf[z, y, :, :, 16:64, :] = nn(swap, jnp.concatenate(parts, axis=0)).astype(BF16).reshape(2, 2, 48, D)
+        buf[z, y] = nn(swap, jnp.concatenate(parts, axis=0)).astype(BF16).reshape(2, 2, 48, D)
         return carry
 
     lax.fori_loop(0, 8, body, 0)
@@ -605,49 +602,99 @@
     ]
 
 
-def scatter_kernel(gqkv, gout, gup, gdown, gsmall, oqkv, oout, oup, odown, osmall, *scratch):
-    ba, bb, (ssem, rsem) = scratch[:6], scratch[6:12], scratch[12:]
+def together(tok_hbm, cot_hbm, fqkv, fout, fup, fdown, fsmall, oqkv, oout, oup, odown, osmall, **refs):
+    gbuf, flat, stage, ssem, rsem, csem = (refs.pop(k) for k in ("gbuf", "flat", "stage", "ssem", "rsem", "csem"))
+    scratch = lambda name: [refs.pop(name + str(i)) for i in range(6)]
+    sets = {name: scratch(name) for name in "abs"}
+    layer = Layer(**refs)
+    rows = layer.rows_count
     at = Place()
+    tok_copy = pltpu.make_async_copy(tok_hbm, layer.tok, csem.at[0])
+    cot_copy = pltpu.make_async_copy(cot_hbm, layer.cot, csem.at[1])
+    tok_copy.start()
+    cot_copy.start()
+    block = gbuf.at[at.z, at.y, at.x, at.c]
+    block[0:16, :] = fsmall[...]
+    pack_share(block, ((16, ((fqkv, 9, 0), (fout, 3, 3))),), flat, stage)
     greet(at)
+    ga = Gather(gbuf, pl.ds(0, 64), ssem.at[0], rsem.at[0], at)
+    gb = Gather(gbuf, pl.ds(64, 96), ssem.at[1], rsem.at[1], at)
+    sb = Scatter(*sets["b"], 96, ssem.at[2], rsem.at[2], at)
+    sa = Scatter(*sets["a"], 48, ssem.at[3], rsem.at[3], at)
+    ss = Scatter(*sets["s"], 16, ssem.at[4], rsem.at[4], at)
+    ga.step0()
+    pack_share(block, ((64, ((fup, 12, 0),)),), flat, stage)
+    pack_down(block, fdown, flat)
     swap = swap_matrix()
-    sa = Scatter(*ba, 64, ssem.at[0], rsem.at[0], at)
-    sb = Scatter(*bb, 96, ssem.at[1], rsem.at[1], at)
-    pack_grads_b(bb[0], gup, gdown, swap, 0)
+    tok_copy.wait()
+    layer.loop(rows // R1, layer.norm_one, ((3, ga.step1), (6, gb.step0)))
+    layer.margins()
+    layer.loop(rows // 128, layer.segments)
+    ga.step2()
+    layer.clear()
+    ga.step3()
+    layer.loop((rows + 2 * MARGIN) // 16, layer.clear_rows)
+    ga.step4()
+    unpack_a(gbuf, swap, layer.wqkv, layer.wout)
+    layer.small[...] = small_table(gbuf[:, :, :, :, 0, :].reshape(32, D))
+    gb.step1()
+    layer.loop(rows // R1, layer.project)
+    layer.loop(layer.tiles, layer.attend, ((2, gb.step2), (7, gb.step3), (12, gb.step4)))
+    unpack_b(gbuf, swap, layer.wup, layer.wdown)
+    cot_copy.wait()
+    layer.loop(rows // R3, layer.feed)
+    pack_grads_b(sets["b"][0], layer.gup, layer.gdown, swap, 0)
     sb.step0()
-    pack_grads_a(ba[0], gqkv, gout, gsmall, swap)
+
+    def finish_b():
+        total = sb.step4()
+        unpack_rows(total, 0, 12, 0, oup)
+        unpack_down(total, 48, odown)
+
+    layer.loop(layer.tiles, layer.attend_back, ((3, sb.step1), (6, sb.step2), (10, sb.step3), (14, finish_b)))
+    layer.loop(rows // R5, layer.project_grad)
+    pack_grads_a(sets["a"][0], layer.gqkv, layer.gout, swap)
     sa.step0()
-    sb.step1()
-    sa.step1()
-    sb.step2()
+    layer.loop(rows // R5, layer.project_back, ((3, sa.step1),))
+    pack_grads_small(sets["s"][0], layer.gsmall)
+    ss.step0()
     sa.step2()
-    sb.step3()
+    ss.step1()
     sa.step3()
-    tb = sb.step4()
-    unpack_rows(tb, 0, 12, 0, oup)
-    unpack_down(tb, 48, odown)
-    ta = sa.step4()
-    unpack_rows(ta, 16, 9, 0, oqkv)
-    unpack_rows(ta, 16, 3, 3, oout)
-    osmall[...] = ta[0:8, :]
-
-
-def run_scatter(gqkv, gout, gup, gdown, gsmall):
-    sds = jax.ShapeDtypeStruct
-    vm = pl.BlockSpec(memory_space=pltpu.VMEM)
-    return pl.pallas_call(
-        scatter_kernel,
-        out_shape=(
-            sds((108, 128), F32), sds((36, 128), F32), sds((144, 128), F32), sds((144, 128), F32), sds((8, D), F32),
-        ),
-        in_specs=[vm] * 5,
-        out_specs=(vm,) * 5,
-        scratch_shapes=scatter_scratch(64) + scatter_scratch(96) + [
-            pltpu.SemaphoreType.DMA((2, NSEM)),
-            pltpu.SemaphoreType.DMA((2, NSEM)),
-        ],
-        compiler_params=pltpu.CompilerParams(vmem_limit_bytes=48 << 20, collective_id=1, has_side_effects=True),
-        name="scatter_grads",
-    )(gqkv, gout, gup, gdown, gsmall)
+    ss.step2()
+    ss.step3()
+    total = sa.step4()
+    unpack_rows(total, 0, 9, 0, oqkv)
+    unpack_rows(total, 0, 3, 3, oout)
+    osmall[...] = ss.step4()[0:8, :]
+
+
+def run_together(tok, cot, lens, segr, fqkv, fout, fup, fdown, fsmall):
+    rows = tok.shape[0]
+    vm, hbm = pltpu.VMEM, pl.ANY
+    ins = dict(
+        tok_hbm=(tok, hbm), cot_hbm=(cot, hbm), lens=(lens, vm), segr=(segr, vm), fqkv=(fqkv, vm), fout=(fout, vm),
+        fup=(fup, vm), fdown=(fdown, vm), fsmall=(fsmall, vm),
+    )
+    outs = dict(
+        out=((rows, D), BF16), ingrad=((rows, D), BF16), oqkv=(fqkv.shape, F32), oout=(fout.shape, F32),
+        oup=(fup.shape, F32), odown=(fdown.shape, F32), osmall=((8, D), F32),
+    )
+    scratch = layer_scratch(rows) | dict(
+        tok=vm((rows, D), BF16), cot=vm((rows, D), BF16), wqkv=vm((D, 3 * D), BF16), wout=vm((D, D), BF16),
+        wup=vm((D, FF), BF16), wdown=vm((FF, D), BF16), small=vm((SMALL_ROWS, D), F32), gqkv=vm((D, 3 * D), F32),
+        gout=vm((D, D), F32), gup=vm((D, FF), F32), gdown=vm((FF, D), F32), gsmall=vm((SMALL_ROWS, D), F32),
+        gbuf=vm((4, 2, 2, 2, BLOCK, D), BF16), flat=vm((144, 128), F32), stage=vm((48, D), F32),
+        ssem=pltpu.SemaphoreType.DMA((5, NSEM)), rsem=pltpu.SemaphoreType.DMA((5, NSEM)),
+        csem=pltpu.SemaphoreType.DMA((2,)),
+    )
+    for name, n in (("a", 48), ("b", 96), ("s", 16)):
+        scratch |= {name + str(i): ref for i, ref in enumerate(scatter_scratch(n))}
+    return named_call(
+        together, ins, {k: (v, vm) for k, v in outs.items()}, scratch,
+        compiler_params=pltpu.CompilerParams(vmem_limit_bytes=63 << 20, collective_id=0, has_side_effects=True),
+        name="layer_and_transfers",
+    )
 
 
 def lanes(flat):
@@ -657,9 +704,9 @@
 def local_direct(tokens, cotangent, image_lengths, segment_ids, w_qkv, w_out, w_up, w_down, small_params):
     share = small_params.shape[0]
     fsmall = jnp.pad(small_params.reshape(1, share), ((0, 15), (0, D - share)))
-    weights = run_gather(lanes(w_qkv), lanes(w_out), lanes(w_up), lanes(w_down), fsmall)
-    out, ingrad, *grads = run_compute(tokens, cotangent, image_lengths, segment_ids.reshape(-1, 128), *weights)
-    oqkv, oout, oup, odown, osmall = run_scatter(*grads)
+    out, ingrad, oqkv, oout, oup, odown, osmall = run_together(
+        tokens, cotangent, image_lengths, lanes(segment_ids), lanes(w_qkv), lanes(w_out), lanes(w_up), lanes(w_down), fsmall
+    )
     return out, ingrad, oqkv.reshape(-1), oout.reshape(-1), oup.reshape(-1), odown.reshape(-1), osmall[0, :share]
 
 
@@ -672,7 +719,7 @@
     wup = gather(w_up).reshape(D, FF)
     wdown = gather(w_down).reshape(FF, D)
     small = jnp.pad(gather(small_params).astype(F32).reshape(-1, D), ((0, SMALL_ROWS - 12), (0, 0)))
-    out, ingrad, gqkv, gout, gup, gdown, gsmall = run_compute(
+    out, ingrad, gqkv, gout, gup, gdown, gsmall = run_alone(
         tokens, cotangent, image_lengths, segment_ids.reshape(-1, 128), wqkv, wout, wup, wdown, small
     )
     return (

time: 184 us -> 152 us (0.83)
  Pallas kernels: 167 us -> 142 us
  local copies, waits for them, and re-layouts: 16 us -> 9.03 us
    pallas_call x3 -> x1, Pallas kernels: 167 us -> 142 us  [named_call(): pl.pallas_call(kernel, out_shape=tuple((jax.ShapeDtypeStruct(*shape) for...]
    unnamed x30 -> x16, local copies, waits for them, and re-layouts: 14.8 us -> 6.5 us
where the time goes in v3:
time: 152 us
  Pallas kernels  142 us (93%)
  local copies, waits for them, and re-layouts  9.03 us (6%)
    pallas_call x1, Pallas kernels, named_call(): pl.pallas_call(kernel, out_shape=tuple((jax.ShapeDtypeStruct(*shape) for...  142 us
    unnamed x16, local copies, waits for them, and re-layouts  6.5 us

profile of v3, /device:TPU:0, one launch (start us, length us, event | category | flops | bytes accessed | tf_op | source)
XLA Modules:
  0.0 151.6 jit_solution(9816140978864825031)
XLA Ops:
  0.6 0.7 reshape.49
  1.3 0.6 pad.4.refs_8_
  1.9 141.9 %layer_and_transfers.1 = (bf16[2048,384]{1,0:T(8,128)(2,1)}, bf16[2048,384]{1,0:T(8,128)(2,1)}, f32[108,128]{1,0:T(8,128)}, f32[36,128]{1,0:T(8,128)}, f32[144,1...) custom-call(bf16[2048,384]{1,0:T(8,128)(2,1)} %refs_0_.1, bf16[2048,384]{1,0:T(8,128)(2,1)} %refs_1_.1, ...), custom_call_target="tpu_custom_call" | custom-call | tf_op jit(solution)/shard_map/layer_and_transfers/pallas_call | solution.py:260
  143.8 1.3 slice.3
  145.0 0.0 copy-start
  145.0 2.8 %copy.22 = bf16[2048,384]{1,0:T(8,128)(2,1)} copy(bf16[2048,384]{1,0:T(8,128)(2,1)} %get-tuple-element.28) | data formatting | bytes 3145728
  147.9 0.0 copy-done
  147.9 0.0 copy-start.3
  147.9 0.0 copy-start.4
  147.9 0.0 copy-start.2
  147.9 0.0 copy-start.1
  147.9 1.1 copy.23
  149.0 0.0 copy-done.3
  149.0 0.6 copy.24
  149.7 0.0 copy-done.4
  149.7 0.6 copy.25
  150.3 0.0 copy-done.2
  150.3 0.6 copy.26
  150.9 0.0 copy-done.1
  150.9 0.6 copy.27
Async XLA Ops:
  145.0 2.8 %copy-start = (bf16[2048,384]{1,0:T(8,128)(2,1)S(1)}, bf16[2048,384]{1,0:T(8,128)(2,1)}, u32[]{:S(2)}) copy-start(bf16[2048,384]{1,0:T(8,128)(2,1)} %get-tuple-element.29) | copy-start | bytes 4718596
  147.9 1.2 copy-start.3
  147.9 1.8 %copy-start.4 = (f32[36,128]{1,0:T(8,128)S(1)}, f32[36,128]{1,0:T(8,128)}, u32[]{:S(2)}) copy-start(f32[36,128]{1,0:T(8,128)} %get-tuple-element.17) | copy-start | bytes 55300
  147.9 2.4 %copy-start.2 = (f32[144,128]{1,0:T(8,128)S(1)}, f32[144,128]{1,0:T(8,128)}, u32[]{:S(2)}) copy-start(f32[144,128]{1,0:T(8,128)} %get-tuple-element.18) | copy-start | bytes 221188
  147.9 3.0 %copy-start.1 = (f32[144,128]{1,0:T(8,128)S(1)}, f32[144,128]{1,0:T(8,128)}, u32[]{:S(2)}) copy-start(f32[144,128]{1,0:T(8,128)} %get-tuple-element.19) | copy-start | bytes 221188
